TPU v7x, 32 devices: a whole 2x2x4 slice. The times are simulated.
32 devices in a mesh: dp: 8 (over y, x, core), rep: 4 (over z).
Axes of the slice: x: 2, y: 2, z: 4, core: 2. Of those that a mesh axis runs over, the one named last changes fastest.
Arguments:
- tokens: bfloat16 [4096, 2048], P(('dp', 'rep')), may hold values from -6 to 6
- cotangent: bfloat16 [4096, 2048], P(('dp', 'rep')), may hold values from -0.125 to 0.125
- doc_ids: int32 [64, 64], P(('dp', 'rep')), may hold values from 0 to 3, never falling along the last dimension, each value on 1 to 32 neighbouring positions
- valid_len: int32 [64], P(('dp', 'rep')), may hold values from 16 to 64
- w_qkv: bfloat16 [2048, 384], P('dp'), may hold values from -0.125 to 0.125
- w_out: bfloat16 [2048, 128], P('dp'), may hold values from -0.5 to 0.5
- norm_gain: bfloat16 [2048], P('dp'), may hold values from 0.5 to 1.5
Outputs:
- grad_qkv: float32 [2048, 384], P('dp')
- grad_out: float32 [2048, 128], P('dp')
- grad_gain: float32 [2048], P('dp')
Inputs may be any that keep to these rules, and one draw needn't show every extreme that they name: `doc_ids`: within each row of 64 positions the ids never fall, and a document has 1 to 32 positions.
All inputs are finite; a program needn't handle non-finite values.
Results may differ from a plain program's by a relative error of at most 0.0079.
Values may be sent and summed in bfloat16 or wider, within the bound.
A program may use at most 64 MiB of HBM per device.

v0:
```python
import functools
import itertools
import math

import jax
import jax.numpy as jnp
from jax import lax
from jax.experimental import pallas as pl
from jax.experimental.pallas import tpu as pltpu
from jax.sharding import PartitionSpec as P

NORM_EPS = 1e-06
ROPE_BASE = 1000000.0


def rotate(vector):
    half_size = vector.shape[-1] // 2
    return jnp.concatenate([-vector[..., half_size:], vector[..., :half_size]], axis=-1)


def unrotate(vector):
    half_size = vector.shape[-1] // 2
    return jnp.concatenate([vector[..., half_size:], -vector[..., :half_size]], axis=-1)


def tables(doc_rows, head_size):
    seq_length = doc_rows.shape[1]
    earlier = jnp.sum((doc_rows[:, None, :] < doc_rows[:, :, None]).astype(jnp.int32), axis=2)
    offsets = (jnp.arange(seq_length, dtype=jnp.int32)[None, :] - earlier).astype(jnp.float32)
    frequency = ROPE_BASE ** (-2.0 * jnp.arange(head_size // 2, dtype=jnp.float32) / head_size)
    angles = offsets[:, :, None] * frequency
    angles = jnp.concatenate([angles, angles], axis=2)
    return (jnp.cos(angles), jnp.sin(angles))


def forward_pass(inputs, doc_rows, w_qkv_full, gain_full):
    batches, seq_length, model_width = inputs.shape
    head_size = w_qkv_full.shape[1] // 3
    scale = 1.0 / math.sqrt(head_size)
    wide_in = inputs.astype(jnp.float32)
    inverse_rms = lax.rsqrt(jnp.mean(wide_in * wide_in, axis=2, keepdims=True) + NORM_EPS)
    scaled_in = wide_in * inverse_rms
    normed = (scaled_in * gain_full.astype(jnp.float32)).astype(jnp.bfloat16)
    projected = jnp.dot(
        normed.reshape(-1, model_width), w_qkv_full, preferred_element_type=jnp.float32
    )
    projected = projected.reshape(batches, seq_length, 3 * head_size)
    cosine, sine_part = tables(doc_rows, head_size)
    queries = projected[:, :, :head_size]
    keys_raw = projected[:, :, head_size : 2 * head_size]
    values_raw = projected[:, :, 2 * head_size :]
    query_rot = ((queries * cosine + rotate(queries) * sine_part) * scale).astype(jnp.bfloat16)
    key_rot = (keys_raw * cosine + rotate(keys_raw) * sine_part).astype(jnp.bfloat16)
    values = values_raw.astype(jnp.bfloat16)
    scores = jnp.einsum("msh,mth->mst", query_rot, key_rot, preferred_element_type=jnp.float32)
    order_row = jnp.arange(seq_length, dtype=jnp.int32)[:, None]
    order_col = jnp.arange(seq_length, dtype=jnp.int32)[None, :]
    allowed = (doc_rows[:, :, None] == doc_rows[:, None, :]) & (order_col <= order_row)[None]
    raised = jnp.where(allowed, jnp.exp(scores), 0.0)
    probabilities = raised / jnp.sum(raised, axis=2, keepdims=True)
    probs_low = probabilities.astype(jnp.bfloat16)
    attended = jnp.einsum(
        "mst,mth->msh", probs_low, values, preferred_element_type=jnp.float32
    ).astype(jnp.bfloat16)
    return (
        scaled_in,
        normed,
        query_rot,
        key_rot,
        values,
        probabilities,
        probs_low,
        attended,
        cosine,
        sine_part,
    )


def backward_pass(saved, live_dy, w_qkv_full, w_out_full):
    (
        scaled_in,
        normed,
        query_rot,
        key_rot,
        values,
        probabilities,
        probs_low,
        attended,
        cosine,
        sine_part,
    ) = saved
    batches, seq_length, model_width = live_dy.shape
    head_size = w_out_full.shape[1]
    scale = 1.0 / math.sqrt(head_size)
    d_attended = jnp.dot(
        live_dy.reshape(-1, model_width), w_out_full, preferred_element_type=jnp.float32
    )
    d_attended = d_attended.reshape(batches, seq_length, head_size).astype(jnp.bfloat16)
    d_probs = jnp.einsum("msh,mth->mst", d_attended, values, preferred_element_type=jnp.float32)
    d_values = jnp.einsum("mst,msh->mth", probs_low, d_attended, preferred_element_type=jnp.float32)
    d_scores = (
        probabilities * (d_probs - jnp.sum(probabilities * d_probs, axis=2, keepdims=True))
    ).astype(jnp.bfloat16)
    d_query = (
        jnp.einsum("mst,mth->msh", d_scores, key_rot, preferred_element_type=jnp.float32) * scale
    )
    d_key = jnp.einsum("mst,msh->mth", d_scores, query_rot, preferred_element_type=jnp.float32)
    d_query = d_query * cosine + unrotate(d_query * sine_part)
    d_key = d_key * cosine + unrotate(d_key * sine_part)
    d_qkv = jnp.concatenate([d_query, d_key, d_values], axis=2).astype(jnp.bfloat16)
    d_normed = lax.dot_general(
        d_qkv.reshape(-1, 3 * head_size),
        w_qkv_full,
        (((1,), (1,)), ((), ())),
        preferred_element_type=jnp.float32,
    )
    gain_term = jnp.sum(d_normed * scaled_in.reshape(-1, model_width), axis=0)
    return (d_qkv, gain_term)


def shards(tokens, cotangent, doc_ids, valid_len, w_qkv, w_out, norm_gain):
    batches, seq_length = doc_ids.shape
    model_width = tokens.shape[1]
    inputs = tokens.reshape(batches, seq_length, model_width)
    live_rows = jnp.arange(seq_length, dtype=jnp.int32)[None, :] < valid_len[:, None]
    live_dy = jnp.where(
        live_rows[:, :, None],
        cotangent.reshape(batches, seq_length, model_width),
        jnp.zeros((), jnp.bfloat16),
    )
    full_set = (
        lax.all_gather(w_qkv, "dp", axis=0, tiled=True),
        lax.all_gather(w_out, "dp", axis=0, tiled=True),
        lax.all_gather(norm_gain, "dp", axis=0, tiled=True),
    )
    saved = forward_pass(inputs, doc_ids, full_set[0], full_set[2])
    qkv_all, gain_total = backward_pass(saved, live_dy, full_set[0], full_set[1])
    normed_all = saved[1]
    attended_all = saved[7]
    head_size = w_out.shape[1]
    normed_flat = normed_all.reshape(-1, model_width)
    qkv_flat = qkv_all.reshape(-1, 3 * head_size)
    attended_flat = attended_all.reshape(-1, head_size)
    grad_qkv = lax.dot_general(
        normed_flat, qkv_flat, (((0,), (0,)), ((), ())), preferred_element_type=jnp.float32
    )
    grad_out = lax.dot_general(
        live_dy.reshape(-1, model_width),
        attended_flat,
        (((0,), (0,)), ((), ())),
        preferred_element_type=jnp.float32,
    )
    shares = (
        lax.psum_scatter(grad_qkv, "dp", scatter_dimension=0, tiled=True),
        lax.psum_scatter(grad_out, "dp", scatter_dimension=0, tiled=True),
    )
    shares = lax.psum((shares[0], shares[1]), "rep")
    gain_whole = lax.psum(gain_total, ("dp", "rep"))
    owned_rows = w_qkv.shape[0]
    gain_start = lax.axis_index("dp") * owned_rows
    gain_owned = lax.dynamic_slice_in_dim(gain_whole, gain_start, owned_rows, 0)
    replicas = lax.axis_size("rep")
    return (shares[0] / replicas, shares[1] / replicas, gain_owned / replicas)


MESH = pl.DeviceIdType.MESH
LANES = 128
CORES = 2


def mm(left, right, dims):
    return lax.dot_general(left, right, (dims, ((), ())), preferred_element_type=jnp.float32)


def eye(size):
    return lax.broadcasted_iota(jnp.int32, (size, size), 0) == lax.broadcasted_iota(
        jnp.int32, (size, size), 1
    )


def to_column(row):
    return jnp.sum(jnp.where(eye(row.shape[1]), row, 0.0), axis=1, keepdims=True)


def to_row(column):
    return jnp.sum(jnp.where(eye(column.shape[0]), column, 0.0), axis=0, keepdims=True)


def fused(
    n,
    replicas,
    x_ref,
    dy_ref,
    doc_ref,
    valid_ref,
    wq_ref,
    wo_ref,
    gain_ref,
    gq_ref,
    go_ref,
    gg_ref,
    w_all,
    gain_all,
    x_all,
    dy_all,
    y_all,
    acc,
    rs_send,
    rs_recv,
    g_all,
    w_send_sem,
    w_recv_sem,
    s_send_sem,
    s_recv_sem,
    a_send_sem,
    a_recv_sem,
    y_send_sem,
    y_recv_sem,
    r_send_sem,
    r_recv_sem,
    g_send_sem,
    g_recv_sem,
):
    me = lax.axis_index("dp")
    rep = lax.axis_index("rep")
    chip, core = me // CORES, lax.rem(me, CORES)
    sibling = chip * CORES + (1 - core)
    rows, width = x_ref.shape
    owned = wq_ref.shape[0]
    head = wo_ref.shape[1]
    wide = 3 * head
    samples, seq = doc_ref.shape
    piece = owned // replicas
    scale = 1.0 / math.sqrt(head)

    barrier = pltpu.get_barrier_semaphore()
    for off in range(1, n):
        pl.semaphore_signal(
            barrier, inc=1, device_id={"dp": lax.rem(me + off, n)}, device_id_type=MESH
        )
    for off in range(1, replicas):
        pl.semaphore_signal(
            barrier,
            inc=1,
            device_id={"rep": lax.rem(rep + off, replicas)},
            device_id_type=MESH,
        )

    gain_row = gain_ref[...].astype(jnp.float32)
    gain_col = to_column(gain_row)
    gain_all[me] = jnp.broadcast_to(gain_row, gain_all.shape[1:])
    my_w = pl.ds(pl.multiple_of(me * owned, LANES), owned)
    w_all[my_w, :wide] = wq_ref[...]
    w_all[my_w, wide:] = wo_ref[...]

    pl.semaphore_wait(barrier, n - 1 + replicas - 1)

    pending = []

    def send(src, dst, send_sem, recv_sem, where):
        copy = pltpu.make_async_remote_copy(
            src_ref=src,
            dst_ref=dst,
            send_sem=send_sem,
            recv_sem=recv_sem,
            device_id=where,
            device_id_type=MESH,
        )
        copy.start()
        pending.append(copy)
        return copy

    along, across = lax.rem(chip, 2), chip // 2
    by_x = across * 2 + 1 - along
    by_y = (1 - across) * 2 + along
    first = by_x + core * (by_y - by_x)
    second = by_y + core * (by_x - by_y)
    far = 3 - chip
    owners = (
        first * CORES + core,
        second * CORES + core,
        far * CORES + core,
        sibling,
        second * CORES + 1 - core,
        first * CORES + 1 - core,
        far * CORES + 1 - core,
    )

    def spread(buf, block, send_sem, recv_sem):
        def part(slot):
            start = pl.multiple_of(owners[slot] * block, LANES)
            return buf.at[pl.ds(start, block)]

        def copy(source, slot, device):
            return send(
                source, source, send_sem.at[slot], recv_sem.at[slot], {"dp": device}
            )

        mine = buf.at[pl.ds(pl.multiple_of(me * block, LANES), block)]
        straight = copy(mine, 0, owners[0])
        straight_second = copy(mine, 1, owners[1])
        passed = copy(mine, 3, sibling)
        yield None
        passed.wait_recv()
        yield owners[3]
        straight.wait_recv()
        relayed = copy(part(0), 2, owners[1])
        passed_first = copy(part(0), 4, sibling)
        yield owners[0]
        straight_second.wait_recv()
        passed_second = copy(part(1), 5, sibling)
        yield owners[1]
        passed_first.wait_recv()
        yield owners[4]
        passed_second.wait_recv()
        yield owners[5]
        relayed.wait_recv()
        passed_far = copy(part(2), 6, sibling)
        yield owners[2]
        passed_far.wait_recv()
        yield owners[6]

    arrivals = spread(w_all, owned, w_send_sem, w_recv_sem)
    next(arrivals)
    gains = {}
    for off in range(1, n):
        gains[off] = send(
            gain_all.at[me],
            gain_all.at[me],
            s_send_sem.at[off],
            s_recv_sem.at[off],
            {"dp": lax.rem(me + off, n)},
        )

    wide_in = x_ref[...].astype(jnp.float32)
    inverse = lax.rsqrt(
        jnp.sum(wide_in * wide_in, axis=1, keepdims=True) * (1.0 / width) + NORM_EPS
    )
    keys, live = [], []
    for m in range(samples):
        doc_row = doc_ref[m : m + 1, :].astype(jnp.float32)
        keys.append(to_column(doc_row) + float(m * seq))
        place = lax.broadcasted_iota(jnp.int32, (seq, 1), 0)
        live.append(jnp.where(place < valid_ref[m], 1.0, 0.0))
    key_col = jnp.concatenate(keys, axis=0)
    live_col = jnp.concatenate(live, axis=0)
    key_row = to_row(key_col)
    earlier = jnp.sum(jnp.where(key_row < key_col, 1.0, 0.0), axis=1, keepdims=True)
    order_row = lax.broadcasted_iota(jnp.int32, (rows, rows), 0)
    order_col = lax.broadcasted_iota(jnp.int32, (rows, rows), 1)
    allowed = (key_row == key_col) & (order_col <= order_row)
    offsets = lax.broadcasted_iota(jnp.int32, (rows, 1), 0).astype(jnp.float32) - earlier
    lane = lax.broadcasted_iota(jnp.int32, (1, head), 1)
    half = lax.rem(lane, head // 2).astype(jnp.float32)
    frequency = jnp.exp(half * (-2.0 / head * math.log(ROPE_BASE)))
    angles = offsets * frequency
    cosine = jnp.cos(angles)
    signed = jnp.sin(angles) * jnp.where(lane < head // 2, -1.0, 1.0)

    def times(source, total):
        cols = pl.ds(pl.multiple_of(source * owned, LANES), owned)
        scaled = x_ref[:, cols].astype(jnp.float32) * inverse
        normed = (scaled * gain_all[source][0:1]).astype(jnp.bfloat16)
        projected = mm(normed, w_all[cols, :wide], ((1,), (0,)))
        d_att = mm(dy_ref[:, cols], w_all[cols, wide:], ((1,), (0,)))
        if total is None:
            return projected, d_att
        return total[0] + projected, total[1] + d_att

    total = times(me, None)
    for off in range(1, n):
        gains[off].wait_recv()
    for source in itertools.islice(arrivals, n - 2):
        total = times(source, total)

    my_rows = pl.ds(pl.multiple_of(me * rows, LANES), rows)
    columns = {}
    for off in range(1, n):
        peer = lax.rem(me + off, n)
        cols = pl.ds(pl.multiple_of(peer * owned, LANES), owned)
        columns[off] = (
            send(
                x_ref.at[:, cols],
                x_all.at[my_rows],
                a_send_sem.at[0, off],
                a_recv_sem.at[0, off],
                {"dp": peer},
            ),
            send(
                dy_ref.at[:, cols],
                dy_all.at[my_rows],
                a_send_sem.at[1, off],
                a_recv_sem.at[1, off],
                {"dp": peer},
            ),
        )

    for source in arrivals:
        total = times(source, total)

    projected = total[0]
    d_att = (total[1] * live_col).astype(jnp.bfloat16)

    def turn(vector, sine_part):
        return vector * cosine + pltpu.roll(vector, head // 2, 1) * sine_part

    query = (turn(projected[:, :head], signed) * scale).astype(jnp.bfloat16)
    key = turn(projected[:, head : 2 * head], signed).astype(jnp.bfloat16)
    values = projected[:, 2 * head :].astype(jnp.bfloat16)
    scores = mm(query, key, ((1,), (1,)))
    raised = jnp.where(allowed, jnp.exp(scores), 0.0)
    probs = raised / jnp.sum(raised, axis=1, keepdims=True)
    probs_low = probs.astype(jnp.bfloat16)
    attended = mm(probs_low, values, ((1,), (0,)))
    d_probs = mm(d_att, values, ((1,), (1,)))
    d_values = mm(probs_low, d_att, ((0,), (0,)))
    d_scores = (
        probs * (d_probs - jnp.sum(probs * d_probs, axis=1, keepdims=True))
    ).astype(jnp.bfloat16)
    d_query = turn(mm(d_scores, key, ((1,), (0,))) * scale, -signed)
    d_key = turn(mm(d_scores, query, ((0,), (0,))), -signed)
    y_all[my_rows, :head] = (d_query * inverse).astype(jnp.bfloat16)
    y_all[my_rows, head : 2 * head] = (d_key * inverse).astype(jnp.bfloat16)
    y_all[my_rows, 2 * head : wide] = (d_values * inverse).astype(jnp.bfloat16)
    y_all[my_rows, wide:] = (attended * live_col).astype(jnp.bfloat16)

    arrivals = spread(y_all, rows, y_send_sem, y_recv_sem)
    next(arrivals)

    my_cols = pl.ds(pl.multiple_of(me * owned, LANES), owned)
    acc[:, :wide] = mm(x_ref[:, my_cols], y_all[my_rows, :wide], ((0,), (0,)))
    acc[:, wide:] = mm(dy_ref[:, my_cols], y_all[my_rows, wide:], ((0,), (0,)))
    for off in range(1, n):
        for copy in columns[off]:
            copy.wait_recv()

    def gather(source):
        part = pl.ds(pl.multiple_of(source * rows, LANES), rows)
        acc[:, :wide] += mm(x_all[part, :], y_all[part, :wide], ((0,), (0,)))
        acc[:, wide:] += mm(dy_all[part, :], y_all[part, wide:], ((0,), (0,)))

    for source in arrivals:
        gather(source)

    rs_send[...] = acc[...].astype(jnp.bfloat16)
    sums = []
    for off in range(1, replicas):
        peer = lax.rem(rep + off, replicas)
        part = pl.ds(pl.multiple_of(peer * piece, 16), piece)
        sums.append(
            send(
                rs_send.at[part],
                rs_recv.at[off - 1],
                r_send_sem.at[off],
                r_recv_sem.at[off],
                {"rep": peer},
            )
        )
    mine = pl.ds(pl.multiple_of(rep * piece, 16), piece)
    whole = acc[mine, :]
    for off in range(1, replicas):
        sums[off - 1].wait_recv()
        whole = whole + rs_recv[off - 1].astype(jnp.float32)
    g_all[mine, :] = (whole * (1.0 / replicas)).astype(jnp.bfloat16)
    last = []
    for off in range(1, replicas):
        peer = lax.rem(rep + off, replicas)
        last.append(
            send(
                g_all.at[mine],
                g_all.at[mine],
                g_send_sem.at[off],
                g_recv_sem.at[off],
                {"rep": peer},
            )
        )
    for copy in last:
        copy.wait_recv()
    total_q = g_all[:, :wide].astype(jnp.float32)
    gq_ref[...] = total_q * gain_col
    go_ref[...] = g_all[:, wide:].astype(jnp.float32)
    gg_ref[...] = to_row(
        jnp.sum(total_q * wq_ref[...].astype(jnp.float32), axis=1, keepdims=True)
    )
    for copy in pending:
        copy.wait_send()


def one_kernel(n, replicas, tokens, cotangent, doc_ids, valid_len, w_qkv, w_out, norm_gain):
    rows, width = tokens.shape
    owned, wide = w_qkv.shape
    head = w_out.shape[1]
    vmem = pl.BlockSpec(memory_space=pltpu.VMEM)
    smem = pl.BlockSpec(memory_space=pltpu.SMEM)
    low = jnp.bfloat16
    full = wide + head
    sem = pltpu.SemaphoreType.DMA
    grad_qkv, grad_out, grad_gain = pl.pallas_call(
        functools.partial(fused, n, replicas),
        out_shape=(
            jax.ShapeDtypeStruct((owned, wide), jnp.float32),
            jax.ShapeDtypeStruct((owned, head), jnp.float32),
            jax.ShapeDtypeStruct((1, owned), jnp.float32),
        ),
        in_specs=[vmem, vmem, vmem, smem, vmem, vmem, vmem],
        out_specs=(vmem, vmem, vmem),
        scratch_shapes=[
            pltpu.VMEM((width, full), low),
            pltpu.VMEM((n, 8, owned), jnp.float32),
            pltpu.VMEM((n * rows, owned), low),
            pltpu.VMEM((n * rows, owned), low),
            pltpu.VMEM((n * rows, full), low),
            pltpu.VMEM((owned, full), jnp.float32),
            pltpu.VMEM((owned, full), low),
            pltpu.VMEM((replicas - 1, owned // replicas, full), low),
            pltpu.VMEM((owned, full), low),
            sem((n - 1,)),
            sem((n - 1,)),
            sem((n,)),
            sem((n,)),
            sem((2, n)),
            sem((2, n)),
            sem((n - 1,)),
            sem((n - 1,)),
            sem((replicas,)),
            sem((replicas,)),
            sem((replicas,)),
            sem((replicas,)),
        ],
        compiler_params=pltpu.CompilerParams(
            collective_id=0, has_side_effects=True, vmem_limit_bytes=48 * 1024 * 1024
        ),
    )(tokens, cotangent, doc_ids, valid_len, w_qkv, w_out, norm_gain.reshape(1, owned))
    return grad_qkv, grad_out, grad_gain.reshape(owned)


def shards_or_kernel(
    n, replicas, tokens, cotangent, doc_ids, valid_len, w_qkv, w_out, norm_gain
):
    rows, owned, head = tokens.shape[0], w_qkv.shape[0], w_out.shape[1]
    fits = (
        n == 4 * CORES
        and replicas > 1
        and owned % LANES == 0
        and owned % (16 * replicas) == 0
        and rows % LANES == 0
        and rows * n <= 2048
        and head == LANES
        and doc_ids.shape[1] % 8 == 0
    )
    if not fits:
        return shards(tokens, cotangent, doc_ids, valid_len, w_qkv, w_out, norm_gain)
    return one_kernel(
        n, replicas, tokens, cotangent, doc_ids, valid_len, w_qkv, w_out, norm_gain
    )


def solution(mesh):
    in_specs = (
        P(("dp", "rep"), None),
        P(("dp", "rep"), None),
        P(("dp", "rep"), None),
        P(("dp", "rep")),
        P("dp", None),
        P("dp", None),
        P("dp"),
    )
    out_specs = (P("dp", None), P("dp", None), P("dp"))
    body = functools.partial(shards_or_kernel, mesh.shape["dp"], mesh.shape["rep"])
    return jax.shard_map(body, mesh=mesh, in_specs=in_specs, out_specs=out_specs, check_vma=False)
```

profile of v0, /device:TPU:0, one launch (start us, length us, event | category | flops | bytes accessed | tf_op | source)
XLA Modules:
  0.0 61.1 jit_solution(1820005208150617346)
XLA Ops:
  0.6 0.0 copy-start.5
  0.6 0.0 copy-start.4
  0.7 0.7 %reshape.12.gain_ref = bf16[1,256]{1,0:T(2,128)(2,1)S(1)} reshape(bf16[256]{0:T(256)(128)(2,1)} %param.13) | data formatting | bytes 1024 | tf_op jit(solution)/shard_map/reshape | solution.py:533
  1.3 0.0 copy-done.5
  1.3 0.0 copy-done.4
  1.3 0.0 copy-start
  1.3 1.0 %copy-done = bf16[128,2048]{1,0:T(8,128)(2,1)S(1)} copy-done((bf16[128,2048]{1,0:T(8,128)(2,1)S(1)}, bf16[128,2048]{1,0:T(8,128)(2,1)}, u32[]{:S(2)}) %copy-start) | copy-done | bytes 524312
  2.4 0.0 copy-start.1
  2.4 1.0 %copy-done.1 = bf16[128,2048]{1,0:T(8,128)(2,1)S(1)} copy-done((bf16[128,2048]{1,0:T(8,128)(2,1)S(1)}, bf16[128,2048]{1,0:T(8,128)(2,1)}, u32[]{:S(2)}) %copy-start.1) | copy-done | bytes 524312
  3.4 0.0 copy-start.2
  3.4 0.9 %copy-done.2 = bf16[256,384]{1,0:T(8,128)(2,1)S(1)} copy-done((bf16[256,384]{1,0:T(8,128)(2,1)S(1)}, bf16[256,384]{1,0:T(8,128)(2,1)}, u32[]{:S(2)}) %copy-start.2) | copy-done | bytes 196632
  4.3 0.0 copy-start.3
  4.3 0.8 %copy-done.3 = bf16[256,128]{1,0:T(8,128)(2,1)S(1)} copy-done((bf16[256,128]{1,0:T(8,128)(2,1)S(1)}, bf16[256,128]{1,0:T(8,128)(2,1)}, u32[]{:S(2)}) %copy-start.3) | copy-done | bytes 65560
  5.2 54.0 %shard_map.94 = (f32[256,384]{1,0:T(8,128)S(1)}, f32[256,128]{1,0:T(8,128)S(1)}, f32[1,256]{1,0:T(1,128)S(1)}) custom-call(bf16[128,2048]{1,0:T(8,128)(2,1)S(1)} %copy-done, bf16[128,2048]{1,0:T(8,128)(2,1)S(1)} %copy-done.1, s32[2,64]{1,0:T(2,128)S(1)} %copy-done.4, s32[2]{0:T(128)S(1)} %copy-done.5, bf16[256,384]{1,0:T(8,128)(2,1)S(1)} %copy-done.2, ...), custom_call_target="tpu_custom_call" | custom-call | tf_op jit(solution)/shard_map/pallas_call | solution.py:498
  59.2 0.7 %copy.13 = f32[256,384]{1,0:T(8,128)} copy(f32[256,384]{1,0:T(8,128)S(1)} %get-tuple-element.12) | data formatting | bytes 786432
  59.9 0.7 %copy.14 = f32[256,128]{1,0:T(8,128)} copy(f32[256,128]{1,0:T(8,128)S(1)} %get-tuple-element.13) | data formatting | bytes 262144
  60.6 0.6 copy.15
Async XLA Ops:
  0.6 0.7 %copy-start.5 = (s32[2]{0:T(128)S(1)}, s32[2]{0:T(128)}, u32[]{:S(2)}) copy-start(s32[2]{0:T(128)} %valid_ref.1) | copy-start | bytes 28
  0.6 0.7 %copy-start.4 = (s32[2,64]{1,0:T(2,128)S(1)}, s32[2,64]{1,0:T(2,128)}, u32[]{:S(2)}) copy-start(s32[2,64]{1,0:T(2,128)} %doc_ref.1) | copy-start | bytes 1540
  1.3 1.0 %copy-start = (bf16[128,2048]{1,0:T(8,128)(2,1)S(1)}, bf16[128,2048]{1,0:T(8,128)(2,1)}, u32[]{:S(2)}) copy-start(bf16[128,2048]{1,0:T(8,128)(2,1)} %x_ref.1) | copy-start | bytes 1572868
  2.4 1.0 %copy-start.1 = (bf16[128,2048]{1,0:T(8,128)(2,1)S(1)}, bf16[128,2048]{1,0:T(8,128)(2,1)}, u32[]{:S(2)}) copy-start(bf16[128,2048]{1,0:T(8,128)(2,1)} %dy_ref.1) | copy-start | bytes 1572868
  3.4 0.9 %copy-start.2 = (bf16[256,384]{1,0:T(8,128)(2,1)S(1)}, bf16[256,384]{1,0:T(8,128)(2,1)}, u32[]{:S(2)}) copy-start(bf16[256,384]{1,0:T(8,128)(2,1)} %wq_ref.1) | copy-start | bytes 589828
  4.3 0.8 %copy-start.3 = (bf16[256,128]{1,0:T(8,128)(2,1)S(1)}, bf16[256,128]{1,0:T(8,128)(2,1)}, u32[]{:S(2)}) copy-start(bf16[256,128]{1,0:T(8,128)(2,1)} %wo_ref.1) | copy-start | bytes 196612
where the time goes:
time: 61.4 us; the launch traced here: 61.1 us
  Pallas kernels  54 us (88%)
  local copies, waits for them, and re-layouts  6.49 us (11%)
  between operations  0.66 us (1%)
    pallas_call x1, Pallas kernels, one_kernel(): pl.pallas_call(functools.partial(fused, n, replicas), out_shape=(jax.Shap...  54 us
    unnamed x15, local copies, waits for them, and re-layouts  5.82 us

commit v1 on v0

--- a/solution.py
+++ b/solution.py
@@ -1,5 +1,4 @@
 import functools
-import itertools
 import math
 
 import jax
@@ -189,31 +188,54 @@
 def fused(
     n,
     replicas,
-    x_ref,
-    dy_ref,
-    doc_ref,
-    valid_ref,
-    wq_ref,
-    wo_ref,
-    gain_ref,
+    x_hbm,
+    dy_hbm,
+    doc_hbm,
+    valid_hbm,
+    wq_hbm,
+    wo_hbm,
+    gain_hbm,
     gq_ref,
     go_ref,
     gg_ref,
-    w_all,
+    x_v,
+    dy_v,
+    doc_v,
+    valid_s,
+    gain_v,
+    wq_all,
+    wo_all,
     gain_all,
+    normed,
+    dy_sib,
+    dy_turned,
+    att,
     x_all,
-    dy_all,
-    y_all,
-    acc,
-    rs_send,
-    rs_recv,
-    g_all,
+    x_turned,
+    yv_all,
+    yqk_all,
+    p_send,
+    p_recv,
+    zg_send,
+    zg_recv,
+    zg_all,
+    zv_send,
+    zv_recv,
+    zv_all,
+    zqk_send,
+    zqk_recv,
+    zqk_all,
+    in_sem,
     w_send_sem,
     w_recv_sem,
     s_send_sem,
     s_recv_sem,
     a_send_sem,
     a_recv_sem,
+    d_send_sem,
+    d_recv_sem,
+    p_send_sem,
+    p_recv_sem,
     y_send_sem,
     y_recv_sem,
     r_send_sem,
@@ -225,13 +247,33 @@
     rep = lax.axis_index("rep")
     chip, core = me // CORES, lax.rem(me, CORES)
     sibling = chip * CORES + (1 - core)
-    rows, width = x_ref.shape
-    owned = wq_ref.shape[0]
-    head = wo_ref.shape[1]
-    wide = 3 * head
-    samples, seq = doc_ref.shape
+    rows, width = x_v.shape
+    owned = wq_hbm.shape[0]
+    head = wo_hbm.shape[1]
+    chips = n // CORES
+    samples, seq = doc_v.shape
     piece = owned // replicas
+    half_owned = owned // 2
     scale = 1.0 / math.sqrt(head)
+
+    def block(index, size):
+        return pl.ds(pl.multiple_of(index * size, LANES), size)
+
+    loads = []
+    for slot, (source, target) in enumerate(
+        (
+            (wq_hbm, wq_all.at[block(me, owned)]),
+            (wo_hbm, wo_all.at[block(me, owned)]),
+            (gain_hbm, gain_v),
+            (x_hbm, x_v),
+            (dy_hbm, dy_v),
+            (doc_hbm, doc_v),
+            (valid_hbm, valid_s),
+        )
+    ):
+        load = pltpu.make_async_copy(source, target, in_sem.at[slot])
+        load.start()
+        loads.append(load)
 
     barrier = pltpu.get_barrier_semaphore()
     for off in range(1, n):
@@ -245,15 +287,6 @@
             device_id={"rep": lax.rem(rep + off, replicas)},
             device_id_type=MESH,
         )
-
-    gain_row = gain_ref[...].astype(jnp.float32)
-    gain_col = to_column(gain_row)
-    gain_all[me] = jnp.broadcast_to(gain_row, gain_all.shape[1:])
-    my_w = pl.ds(pl.multiple_of(me * owned, LANES), owned)
-    w_all[my_w, :wide] = wq_ref[...]
-    w_all[my_w, wide:] = wo_ref[...]
-
-    pl.semaphore_wait(barrier, n - 1 + replicas - 1)
 
     pending = []
 
@@ -286,42 +319,34 @@
         far * CORES + 1 - core,
     )
 
-    def spread(buf, block, send_sem, recv_sem):
-        def part(slot):
-            start = pl.multiple_of(owners[slot] * block, LANES)
-            return buf.at[pl.ds(start, block)]
-
-        def copy(source, slot, device):
-            return send(
-                source, source, send_sem.at[slot], recv_sem.at[slot], {"dp": device}
-            )
-
-        mine = buf.at[pl.ds(pl.multiple_of(me * block, LANES), block)]
-        straight = copy(mine, 0, owners[0])
-        straight_second = copy(mine, 1, owners[1])
-        passed = copy(mine, 3, sibling)
-        yield None
-        passed.wait_recv()
-        yield owners[3]
-        straight.wait_recv()
-        relayed = copy(part(0), 2, owners[1])
-        passed_first = copy(part(0), 4, sibling)
-        yield owners[0]
-        straight_second.wait_recv()
-        passed_second = copy(part(1), 5, sibling)
-        yield owners[1]
-        passed_first.wait_recv()
-        yield owners[4]
-        passed_second.wait_recv()
-        yield owners[5]
-        relayed.wait_recv()
-        passed_far = copy(part(2), 6, sibling)
-        yield owners[2]
-        passed_far.wait_recv()
-        yield owners[6]
-
-    arrivals = spread(w_all, owned, w_send_sem, w_recv_sem)
-    next(arrivals)
+    def w_part(owner, part):
+        if part == 2:
+            return wo_all.at[block(owner, owned)]
+        start = pl.multiple_of(owner * owned + part * half_owned, LANES)
+        return wq_all.at[pl.ds(start, half_owned)]
+
+    def w_copy(owner, part, slot, device):
+        source = w_part(owner, part)
+        return send(
+            source,
+            source,
+            w_send_sem.at[slot, part],
+            w_recv_sem.at[slot, part],
+            {"dp": device},
+        )
+
+    loads[2].wait()
+    gain_row = gain_v[...].reshape(1, owned).astype(jnp.float32)
+    gain_all[me] = jnp.broadcast_to(gain_row, gain_all.shape[1:])
+    loads[0].wait()
+    loads[1].wait()
+    pl.semaphore_wait(barrier, n - 1 + replicas - 1)
+
+    w = {}
+    for part in range(2):
+        w[0, part] = w_copy(me, part, 0, owners[0])
+        w[1, part] = w_copy(me, part, 1, owners[1])
+        w[3, part] = w_copy(me, part, 3, sibling)
     gains = {}
     for off in range(1, n):
         gains[off] = send(
@@ -331,17 +356,52 @@
             s_recv_sem.at[off],
             {"dp": lax.rem(me + off, n)},
         )
-
-    wide_in = x_ref[...].astype(jnp.float32)
+    w[0, 2] = w_copy(me, 2, 0, owners[0])
+    w[3, 2] = w_copy(me, 2, 3, sibling)
+
+    loads[4].wait()
+    crossed = []
+    for place in range(chips):
+        crossed.append(
+            send(
+                dy_v.at[:, block(place * CORES + 1 - core, owned)],
+                dy_sib.at[place],
+                d_send_sem.at[place],
+                d_recv_sem.at[place],
+                {"dp": sibling},
+            )
+        )
+
+    loads[3].wait()
+    loads[5].wait()
+    loads[6].wait()
+    gain_col = to_column(gain_row)
+    wide_in = x_v[...].astype(jnp.float32)
     inverse = lax.rsqrt(
         jnp.sum(wide_in * wide_in, axis=1, keepdims=True) * (1.0 / width) + NORM_EPS
     )
+    for off in range(1, n):
+        gains[off].wait_recv()
+    for place in range(n):
+        cols = pl.ds(place * owned, owned)
+        scaled = x_v[:, cols].astype(jnp.float32) * inverse
+        normed[:, cols] = (scaled * gain_all[place][0:1]).astype(jnp.bfloat16)
+
+    def times(source, total):
+        product = mm(normed[:, block(source, owned)], wq_all[block(source, owned), :], ((1,), (0,)))
+        return product if total is None else total + product
+
+    total = times(me, None)
+    w[3, 0].wait_recv()
+    w[3, 1].wait_recv()
+    total = times(sibling, total)
+
     keys, live = [], []
     for m in range(samples):
-        doc_row = doc_ref[m : m + 1, :].astype(jnp.float32)
+        doc_row = doc_v[m : m + 1, :].astype(jnp.float32)
         keys.append(to_column(doc_row) + float(m * seq))
         place = lax.broadcasted_iota(jnp.int32, (seq, 1), 0)
-        live.append(jnp.where(place < valid_ref[m], 1.0, 0.0))
+        live.append(jnp.where(place < valid_s[m], 1.0, 0.0))
     key_col = jnp.concatenate(keys, axis=0)
     live_col = jnp.concatenate(live, axis=0)
     key_row = to_row(key_col)
@@ -357,49 +417,53 @@
     cosine = jnp.cos(angles)
     signed = jnp.sin(angles) * jnp.where(lane < head // 2, -1.0, 1.0)
 
-    def times(source, total):
-        cols = pl.ds(pl.multiple_of(source * owned, LANES), owned)
-        scaled = x_ref[:, cols].astype(jnp.float32) * inverse
-        normed = (scaled * gain_all[source][0:1]).astype(jnp.bfloat16)
-        projected = mm(normed, w_all[cols, :wide], ((1,), (0,)))
-        d_att = mm(dy_ref[:, cols], w_all[cols, wide:], ((1,), (0,)))
-        if total is None:
-            return projected, d_att
-        return total[0] + projected, total[1] + d_att
-
-    total = times(me, None)
-    for off in range(1, n):
-        gains[off].wait_recv()
-    for source in itertools.islice(arrivals, n - 2):
-        total = times(source, total)
-
-    my_rows = pl.ds(pl.multiple_of(me * rows, LANES), rows)
+    for part in range(2):
+        w[0, part].wait_recv()
+        w[2, part] = w_copy(owners[0], part, 2, owners[1])
+        w[4, part] = w_copy(owners[0], part, 4, sibling)
+        w[1, part].wait_recv()
+        w[5, part] = w_copy(owners[1], part, 5, sibling)
+    w[1, 2] = w_copy(me, 2, 1, owners[1])
+
+    for place in range(chips):
+        crossed[place].wait_recv()
+        turned = pl.ds(place * owned, owned)
+        dy_turned[turned, :rows] = dy_v[:, block(place * CORES + core, owned)].T
+        dy_turned[turned, rows:] = dy_sib[place].T
+
+    total = times(owners[0], total)
+    total = times(owners[1], total)
+
+    w[0, 2].wait_recv()
+    w[2, 2] = w_copy(owners[0], 2, 2, owners[1])
+    w[4, 2] = w_copy(owners[0], 2, 4, sibling)
+
+    mine = block(me, rows)
     columns = {}
-    for off in range(1, n):
-        peer = lax.rem(me + off, n)
-        cols = pl.ds(pl.multiple_of(peer * owned, LANES), owned)
-        columns[off] = (
-            send(
-                x_ref.at[:, cols],
-                x_all.at[my_rows],
-                a_send_sem.at[0, off],
-                a_recv_sem.at[0, off],
-                {"dp": peer},
-            ),
-            send(
-                dy_ref.at[:, cols],
-                dy_all.at[my_rows],
-                a_send_sem.at[1, off],
-                a_recv_sem.at[1, off],
-                {"dp": peer},
-            ),
-        )
-
-    for source in arrivals:
-        total = times(source, total)
-
-    projected = total[0]
-    d_att = (total[1] * live_col).astype(jnp.bfloat16)
+    for slot in (2, 0, 1, 6, 5, 4, 3):
+        columns[slot] = send(
+            x_v.at[:, block(owners[slot], owned)],
+            x_all.at[mine],
+            a_send_sem.at[slot],
+            a_recv_sem.at[slot],
+            {"dp": owners[slot]},
+        )
+
+    for slot in (4, 5):
+        for part in range(2):
+            w[slot, part].wait_recv()
+        total = times(owners[slot], total)
+    for part in range(2):
+        w[2, part].wait_recv()
+        w[6, part] = w_copy(owners[2], part, 6, sibling)
+    w[1, 2].wait_recv()
+    w[5, 2] = w_copy(owners[1], 2, 5, sibling)
+    total = times(owners[2], total)
+    w[2, 2].wait_recv()
+    w[6, 2] = w_copy(owners[2], 2, 6, sibling)
+    for part in range(2):
+        w[6, part].wait_recv()
+    projected = times(owners[6], total)
 
     def turn(vector, sine_part):
         return vector * cosine + pltpu.roll(vector, head // 2, 1) * sine_part
@@ -412,125 +476,244 @@
     probs = raised / jnp.sum(raised, axis=1, keepdims=True)
     probs_low = probs.astype(jnp.bfloat16)
     attended = mm(probs_low, values, ((1,), (0,)))
+    att[:rows] = (attended * live_col).astype(jnp.bfloat16)
+    att_copy = send(
+        att.at[:rows],
+        att.at[rows:],
+        d_send_sem.at[chips],
+        d_recv_sem.at[chips],
+        {"dp": sibling},
+    )
+
+    for slot in (3, 4, 5, 6):
+        w[slot, 2].wait_recv()
+    d_att = (mm(dy_v[...], wo_all[...], ((1,), (0,))) * live_col).astype(jnp.bfloat16)
+    att_copy.wait_recv()
+
+    def out_part(owner):
+        return mm(dy_turned[block(owner // CORES, owned), :], att[...], ((1,), (0,)))
+
+    p_copies = []
+    for slot in (2, 0, 1):
+        p_send[slot] = out_part(owners[slot]).astype(jnp.bfloat16)
+        p_copies.append(
+            send(
+                p_send.at[slot],
+                p_recv.at[slot],
+                p_send_sem.at[slot],
+                p_recv_sem.at[slot],
+                {"dp": owners[slot]},
+            )
+        )
+
+    def y_copy(buf, chunk, owner, slot, device):
+        source = buf.at[block(owner, rows)]
+        return send(
+            source,
+            source,
+            y_send_sem.at[chunk, slot],
+            y_recv_sem.at[chunk, slot],
+            {"dp": device},
+        )
+
+    d_values = mm(probs_low, d_att, ((0,), (0,)))
+    yv_all[mine] = (d_values * inverse).astype(jnp.bfloat16)
+    y = {}
+    for slot in (2, 0, 1, 3):
+        y[0, slot] = y_copy(yv_all, 0, me, slot, owners[slot])
     d_probs = mm(d_att, values, ((1,), (1,)))
-    d_values = mm(probs_low, d_att, ((0,), (0,)))
     d_scores = (
         probs * (d_probs - jnp.sum(probs * d_probs, axis=1, keepdims=True))
     ).astype(jnp.bfloat16)
     d_query = turn(mm(d_scores, key, ((1,), (0,))) * scale, -signed)
     d_key = turn(mm(d_scores, query, ((0,), (0,))), -signed)
-    y_all[my_rows, :head] = (d_query * inverse).astype(jnp.bfloat16)
-    y_all[my_rows, head : 2 * head] = (d_key * inverse).astype(jnp.bfloat16)
-    y_all[my_rows, 2 * head : wide] = (d_values * inverse).astype(jnp.bfloat16)
-    y_all[my_rows, wide:] = (attended * live_col).astype(jnp.bfloat16)
-
-    arrivals = spread(y_all, rows, y_send_sem, y_recv_sem)
-    next(arrivals)
-
-    my_cols = pl.ds(pl.multiple_of(me * owned, LANES), owned)
-    acc[:, :wide] = mm(x_ref[:, my_cols], y_all[my_rows, :wide], ((0,), (0,)))
-    acc[:, wide:] = mm(dy_ref[:, my_cols], y_all[my_rows, wide:], ((0,), (0,)))
-    for off in range(1, n):
-        for copy in columns[off]:
-            copy.wait_recv()
-
-    def gather(source):
-        part = pl.ds(pl.multiple_of(source * rows, LANES), rows)
-        acc[:, :wide] += mm(x_all[part, :], y_all[part, :wide], ((0,), (0,)))
-        acc[:, wide:] += mm(dy_all[part, :], y_all[part, wide:], ((0,), (0,)))
-
-    for source in arrivals:
-        gather(source)
-
-    rs_send[...] = acc[...].astype(jnp.bfloat16)
-    sums = []
-    for off in range(1, replicas):
-        peer = lax.rem(rep + off, replicas)
-        part = pl.ds(pl.multiple_of(peer * piece, 16), piece)
-        sums.append(
-            send(
-                rs_send.at[part],
-                rs_recv.at[off - 1],
-                r_send_sem.at[off],
-                r_recv_sem.at[off],
-                {"rep": peer},
+    yqk_all[mine, :head] = (d_query * inverse).astype(jnp.bfloat16)
+    yqk_all[mine, head:] = (d_key * inverse).astype(jnp.bfloat16)
+    for slot in (2, 0, 1, 3):
+        y[1, slot] = y_copy(yqk_all, 1, me, slot, owners[slot])
+
+    out_total = out_part(me)
+    x_turned[:, mine] = x_v[:, block(me, owned)].T
+    for slot, source in enumerate((0, 1, 2, 3, 5, 4, 6)):
+        columns[slot].wait_recv()
+        part = block(owners[source], rows)
+        x_turned[:, part] = x_all[part].T
+
+    my_piece = pl.ds(pl.multiple_of(rep * piece, 16), piece)
+
+    def z_start(chunk, buf, received, total):
+        buf[...] = total.astype(jnp.bfloat16)
+        copies = []
+        for off in range(1, replicas):
+            peer = lax.rem(rep + off, replicas)
+            part = pl.ds(pl.multiple_of(peer * piece, 16), piece)
+            copies.append(
+                send(
+                    buf.at[part],
+                    received.at[off - 1],
+                    r_send_sem.at[chunk, off],
+                    r_recv_sem.at[chunk, off],
+                    {"rep": peer},
+                )
             )
-        )
-    mine = pl.ds(pl.multiple_of(rep * piece, 16), piece)
-    whole = acc[mine, :]
-    for off in range(1, replicas):
-        sums[off - 1].wait_recv()
-        whole = whole + rs_recv[off - 1].astype(jnp.float32)
-    g_all[mine, :] = (whole * (1.0 / replicas)).astype(jnp.bfloat16)
-    last = []
-    for off in range(1, replicas):
-        peer = lax.rem(rep + off, replicas)
-        last.append(
-            send(
-                g_all.at[mine],
-                g_all.at[mine],
-                g_send_sem.at[off],
-                g_recv_sem.at[off],
-                {"rep": peer},
+        return copies
+
+    def z_middle(chunk, buf, received, gathered, copies):
+        whole = buf[my_piece].astype(jnp.float32)
+        for off in range(1, replicas):
+            copies[off - 1].wait_recv()
+            whole = whole + received[off - 1].astype(jnp.float32)
+        gathered[my_piece] = (whole * (1.0 / replicas)).astype(jnp.bfloat16)
+        last = []
+        for off in range(1, replicas):
+            peer = lax.rem(rep + off, replicas)
+            last.append(
+                send(
+                    gathered.at[my_piece],
+                    gathered.at[my_piece],
+                    g_send_sem.at[chunk, off],
+                    g_recv_sem.at[chunk, off],
+                    {"rep": peer},
+                )
             )
-        )
-    for copy in last:
+        return last
+
+    def y_pass(buf, chunk):
+        for slot, onward in ((0, 4), (1, 5), (2, 6)):
+            y[chunk, slot].wait_recv()
+            y[chunk, onward] = y_copy(buf, chunk, owners[slot], onward, sibling)
+
+    y_pass(yv_all, 0)
+    for slot, copy in zip((2, 0, 1), p_copies):
         copy.wait_recv()
-    total_q = g_all[:, :wide].astype(jnp.float32)
-    gq_ref[...] = total_q * gain_col
-    go_ref[...] = g_all[:, wide:].astype(jnp.float32)
-    gg_ref[...] = to_row(
-        jnp.sum(total_q * wq_ref[...].astype(jnp.float32), axis=1, keepdims=True)
-    )
+        out_total = out_total + p_recv[slot].astype(jnp.float32)
+    out_copies = z_start(0, zg_send, zg_recv, out_total)
+    for slot in (3, 4, 5, 6):
+        y[0, slot].wait_recv()
+    value_total = mm(x_turned[...], yv_all[...], ((1,), (0,)))
+    value_copies = z_start(1, zv_send, zv_recv, value_total)
+    y_pass(yqk_all, 1)
+    for slot in (3, 4, 5, 6):
+        y[1, slot].wait_recv()
+    both_total = mm(x_turned[...], yqk_all[...], ((1,), (0,)))
+    both_copies = z_start(2, zqk_send, zqk_recv, both_total)
+
+    out_last = z_middle(0, zg_send, zg_recv, zg_all, out_copies)
+    value_last = z_middle(1, zv_send, zv_recv, zv_all, value_copies)
+    both_last = z_middle(2, zqk_send, zqk_recv, zqk_all, both_copies)
+
+    wq_mine = wq_all.at[block(me, owned)]
+    for copy in out_last:
+        copy.wait_recv()
+    go_ref[...] = zg_all[...].astype(jnp.float32)
+    for copy in value_last:
+        copy.wait_recv()
+    value_sum = zv_all[...].astype(jnp.float32)
+    gq_ref[:, 2 * head :] = value_sum * gain_col
+    gain_sum = value_sum * wq_mine[:, 2 * head :].astype(jnp.float32)
+    for copy in both_last:
+        copy.wait_recv()
+    for place in range(2):
+        cols = pl.ds(place * head, head)
+        both_sum = zqk_all[:, cols].astype(jnp.float32)
+        gq_ref[:, cols] = both_sum * gain_col
+        gain_sum = gain_sum + both_sum * wq_mine[:, cols].astype(jnp.float32)
+    gg_ref[...] = to_row(jnp.sum(gain_sum, axis=1, keepdims=True))
     for copy in pending:
         copy.wait_send()
+
+
+def stored(gq_ref, go_ref, gg_ref, gq_out, go_out, gg_out, sem):
+    copies = []
+    for slot, (source, target) in enumerate(
+        ((gq_ref, gq_out), (go_ref, go_out), (gg_ref, gg_out))
+    ):
+        copy = pltpu.make_async_copy(source, target, sem.at[slot])
+        copy.start()
+        copies.append(copy)
+    for copy in copies:
+        copy.wait()
 
 
 def one_kernel(n, replicas, tokens, cotangent, doc_ids, valid_len, w_qkv, w_out, norm_gain):
     rows, width = tokens.shape
     owned, wide = w_qkv.shape
     head = w_out.shape[1]
+    chips = n // CORES
+    piece = owned // replicas
     vmem = pl.BlockSpec(memory_space=pltpu.VMEM)
-    smem = pl.BlockSpec(memory_space=pltpu.SMEM)
+    anywhere = pl.BlockSpec(memory_space=pl.ANY)
     low = jnp.bfloat16
-    full = wide + head
     sem = pltpu.SemaphoreType.DMA
-    grad_qkv, grad_out, grad_gain = pl.pallas_call(
+    shapes = (
+        jax.ShapeDtypeStruct((owned, wide), jnp.float32),
+        jax.ShapeDtypeStruct((owned, head), jnp.float32),
+        jax.ShapeDtypeStruct((1, owned), jnp.float32),
+    )
+
+    def z_buffers(cols):
+        return [
+            pltpu.VMEM((owned, cols), low),
+            pltpu.VMEM((replicas - 1, piece, cols), low),
+            pltpu.VMEM((owned, cols), low),
+        ]
+
+    grads = pl.pallas_call(
         functools.partial(fused, n, replicas),
-        out_shape=(
-            jax.ShapeDtypeStruct((owned, wide), jnp.float32),
-            jax.ShapeDtypeStruct((owned, head), jnp.float32),
-            jax.ShapeDtypeStruct((1, owned), jnp.float32),
-        ),
-        in_specs=[vmem, vmem, vmem, smem, vmem, vmem, vmem],
+        out_shape=shapes,
+        in_specs=[anywhere] * 7,
         out_specs=(vmem, vmem, vmem),
         scratch_shapes=[
-            pltpu.VMEM((width, full), low),
+            pltpu.VMEM((rows, width), low),
+            pltpu.VMEM((rows, width), low),
+            pltpu.VMEM(doc_ids.shape, jnp.int32),
+            pltpu.SMEM(valid_len.shape, jnp.int32),
+            pltpu.VMEM((owned,), low),
+            pltpu.VMEM((width, wide), low),
+            pltpu.VMEM((width, head), low),
             pltpu.VMEM((n, 8, owned), jnp.float32),
+            pltpu.VMEM((rows, width), low),
+            pltpu.VMEM((chips, rows, owned), low),
+            pltpu.VMEM((chips * owned, CORES * rows), low),
+            pltpu.VMEM((CORES * rows, head), low),
             pltpu.VMEM((n * rows, owned), low),
-            pltpu.VMEM((n * rows, owned), low),
-            pltpu.VMEM((n * rows, full), low),
-            pltpu.VMEM((owned, full), jnp.float32),
-            pltpu.VMEM((owned, full), low),
-            pltpu.VMEM((replicas - 1, owned // replicas, full), low),
-            pltpu.VMEM((owned, full), low),
+            pltpu.VMEM((owned, n * rows), low),
+            pltpu.VMEM((n * rows, head), low),
+            pltpu.VMEM((n * rows, 2 * head), low),
+            pltpu.VMEM((chips - 1, owned, head), low),
+            pltpu.VMEM((chips - 1, owned, head), low),
+            *z_buffers(head),
+            *z_buffers(head),
+            *z_buffers(2 * head),
+            sem((7,)),
+            sem((n - 1, 3)),
+            sem((n - 1, 3)),
+            sem((n,)),
+            sem((n,)),
             sem((n - 1,)),
             sem((n - 1,)),
-            sem((n,)),
-            sem((n,)),
-            sem((2, n)),
-            sem((2, n)),
-            sem((n - 1,)),
-            sem((n - 1,)),
-            sem((replicas,)),
-            sem((replicas,)),
-            sem((replicas,)),
-            sem((replicas,)),
+            sem((chips + 1,)),
+            sem((chips + 1,)),
+            sem((chips - 1,)),
+            sem((chips - 1,)),
+            sem((2, n - 1)),
+            sem((2, n - 1)),
+            sem((3, replicas)),
+            sem((3, replicas)),
+            sem((3, replicas)),
+            sem((3, replicas)),
         ],
         compiler_params=pltpu.CompilerParams(
-            collective_id=0, has_side_effects=True, vmem_limit_bytes=48 * 1024 * 1024
+            collective_id=0, has_side_effects=True, vmem_limit_bytes=60 * 1024 * 1024
         ),
-    )(tokens, cotangent, doc_ids, valid_len, w_qkv, w_out, norm_gain.reshape(1, owned))
+    )(tokens, cotangent, doc_ids, valid_len, w_qkv, w_out, norm_gain)
+    grad_qkv, grad_out, grad_gain = pl.pallas_call(
+        stored,
+        out_shape=shapes,
+        in_specs=[vmem] * 3,
+        out_specs=(anywhere,) * 3,
+        scratch_shapes=[sem((3,))],
+    )(*grads)
     return grad_qkv, grad_out, grad_gain.reshape(owned)
 
 

time: 61.4 us -> 50.4 us (0.82)
  local copies, waits for them, and re-layouts: 6.49 us -> 0 us
  Pallas kernels: 54 us -> 49.6 us
    unnamed x15 -> x0, local copies, waits for them, and re-layouts: 5.82 us -> none
    pallas_call x1 -> x2, Pallas kernels: 54 us -> 49.6 us  [the longest x1 47.7 us: one_kernel(): pl.pallas_call(functools.partial(fused, n, replicas), out_shape=shapes, i...]
    reshape x1 -> x0, local copies, waits for them, and re-layouts: 0.67 us -> none  [one_kernel(): norm_gain.reshape(1, owned)]
where the time goes in v1:
time: 50.4 us; the launch traced here: 50.2 us
  Pallas kernels  49.6 us (98%)
  between operations  0.64 us (1%)
    pallas_call x1, Pallas kernels, one_kernel(): pl.pallas_call(functools.partial(fused, n, replicas), out_shape=shapes, i...  47.7 us
    pallas_call x1, Pallas kernels, one_kernel(): pl.pallas_call(stored, out_shape=shapes, in_specs=[vmem] * 3, out_specs=(...  1.88 us

profile of v1, /device:TPU:0, one launch (start us, length us, event | category | flops | bytes accessed | tf_op | source)
XLA Modules:
  0.0 50.2 jit_solution(18163904158588361759)
XLA Ops:
  0.6 47.7 %shard_map.94 = (f32[256,384]{1,0:T(8,128)}, f32[256,128]{1,0:T(8,128)}, f32[1,256]{1,0:T(1,128)}) custom-call(bf16[128,2048]{1,0:T(8,128)(2,1)} %x_hbm.1, bf16[128,2048]{1,0:T(8,128)(2,1)} %dy_hbm.1, s32[2,64]{1,0:T(2,128)} %doc_hbm.1, s32[2]{0:T(128)} %valid_hbm.1, bf16[256,384]{1,0:T(8,128)(2,1)} %wq_hbm.1, bf16[256,128]{1,0:T(8,128)(2,1)} %wo_hbm.1, ...), custom_call_target="tpu_custom_call" | custom-call | tf_op jit(solution)/shard_map/pallas_call | solution.py:661
  48.4 1.9 %shard_map.95 = (f32[256,384]{1,0:T(8,128)}, f32[256,128]{1,0:T(8,128)}, f32[1,256]{1,0:T(1,128)}) custom-call(f32[256,384]{1,0:T(8,128)} %get-tuple-element.9.gq_ref, f32[256,128]{1,0:T(8,128)} %get-tuple-element.10.go_ref, f32[1,256]{1,0:T(1,128)} %get-tuple-element.11.gg_ref), custom_call_target="tpu_custom_call" | custom-call | tf_op jit(solution)/shard_map/pallas_call | solution.py:710

commit v2 on v1

--- a/solution.py
+++ b/solution.py
@@ -212,19 +212,14 @@
     att,
     x_all,
     x_turned,
-    yv_all,
-    yqk_all,
+    y_all,
     p_send,
     p_recv,
-    zg_send,
-    zg_recv,
-    zg_all,
-    zv_send,
-    zv_recv,
-    zv_all,
-    zqk_send,
-    zqk_recv,
-    zqk_all,
+    q_send,
+    q_recv,
+    z_send,
+    z_recv,
+    z_all,
     in_sem,
     w_send_sem,
     w_recv_sem,
@@ -236,6 +231,8 @@
     d_recv_sem,
     p_send_sem,
     p_recv_sem,
+    q_send_sem,
+    q_recv_sem,
     y_send_sem,
     y_recv_sem,
     r_send_sem,
@@ -337,7 +334,7 @@
 
     loads[2].wait()
     gain_row = gain_v[...].reshape(1, owned).astype(jnp.float32)
-    gain_all[me] = jnp.broadcast_to(gain_row, gain_all.shape[1:])
+    gain_all[me] = gain_row
     loads[0].wait()
     loads[1].wait()
     pl.semaphore_wait(barrier, n - 1 + replicas - 1)
@@ -345,7 +342,7 @@
     w = {}
     for part in range(2):
         w[0, part] = w_copy(me, part, 0, owners[0])
-        w[1, part] = w_copy(me, part, 1, owners[1])
+    for part in range(2):
         w[3, part] = w_copy(me, part, 3, sibling)
     gains = {}
     for off in range(1, n):
@@ -356,7 +353,6 @@
             s_recv_sem.at[off],
             {"dp": lax.rem(me + off, n)},
         )
-    w[0, 2] = w_copy(me, 2, 0, owners[0])
     w[3, 2] = w_copy(me, 2, 3, sibling)
 
     loads[4].wait()
@@ -380,22 +376,6 @@
     inverse = lax.rsqrt(
         jnp.sum(wide_in * wide_in, axis=1, keepdims=True) * (1.0 / width) + NORM_EPS
     )
-    for off in range(1, n):
-        gains[off].wait_recv()
-    for place in range(n):
-        cols = pl.ds(place * owned, owned)
-        scaled = x_v[:, cols].astype(jnp.float32) * inverse
-        normed[:, cols] = (scaled * gain_all[place][0:1]).astype(jnp.bfloat16)
-
-    def times(source, total):
-        product = mm(normed[:, block(source, owned)], wq_all[block(source, owned), :], ((1,), (0,)))
-        return product if total is None else total + product
-
-    total = times(me, None)
-    w[3, 0].wait_recv()
-    w[3, 1].wait_recv()
-    total = times(sibling, total)
-
     keys, live = [], []
     for m in range(samples):
         doc_row = doc_v[m : m + 1, :].astype(jnp.float32)
@@ -418,12 +398,32 @@
     signed = jnp.sin(angles) * jnp.where(lane < head // 2, -1.0, 1.0)
 
     for part in range(2):
+        w[1, part] = w_copy(me, part, 1, owners[1])
+    w[0, 2] = w_copy(me, 2, 0, owners[0])
+    for off in range(1, n):
+        gains[off].wait_recv()
+    for place in range(n):
+        cols = pl.ds(place * owned, owned)
+        scaled = x_v[:, cols].astype(jnp.float32) * inverse
+        normed[:, cols] = (scaled * gain_all[place]).astype(jnp.bfloat16)
+
+    def times(source, total):
+        product = mm(normed[:, block(source, owned)], wq_all[block(source, owned), :], ((1,), (0,)))
+        return product if total is None else total + product
+
+    total = times(me, None)
+    w[3, 0].wait_recv()
+    w[3, 1].wait_recv()
+    total = times(sibling, total)
+
+    for part in range(2):
         w[0, part].wait_recv()
         w[2, part] = w_copy(owners[0], part, 2, owners[1])
         w[4, part] = w_copy(owners[0], part, 4, sibling)
+    w[1, 2] = w_copy(me, 2, 1, owners[1])
+    for part in range(2):
         w[1, part].wait_recv()
         w[5, part] = w_copy(owners[1], part, 5, sibling)
-    w[1, 2] = w_copy(me, 2, 1, owners[1])
 
     for place in range(chips):
         crossed[place].wait_recv()
@@ -490,25 +490,26 @@
     d_att = (mm(dy_v[...], wo_all[...], ((1,), (0,))) * live_col).astype(jnp.bfloat16)
     att_copy.wait_recv()
 
-    def out_part(owner):
-        return mm(dy_turned[block(owner // CORES, owned), :], att[...], ((1,), (0,)))
-
+    by_chip = mm(dy_turned[...], att[...], ((1,), (0,)))
+    p_send[...] = by_chip.reshape(chips, replicas, piece, head).astype(jnp.bfloat16)
     p_copies = []
-    for slot in (2, 0, 1):
-        p_send[slot] = out_part(owners[slot]).astype(jnp.bfloat16)
+    for off in range(1, replicas):
+        peer = lax.rem(rep + off, replicas)
         p_copies.append(
             send(
-                p_send.at[slot],
-                p_recv.at[slot],
-                p_send_sem.at[slot],
-                p_recv_sem.at[slot],
-                {"dp": owners[slot]},
+                p_send.at[:, peer],
+                p_recv.at[off - 1],
+                p_send_sem.at[off],
+                p_recv_sem.at[off],
+                {"rep": peer},
             )
         )
 
-    def y_copy(buf, chunk, owner, slot, device):
-        source = buf.at[block(owner, rows)]
-        return send(
+    y = {}
+
+    def y_copy(chunk, owner, slot, device):
+        source = y_all.at[chunk].at[block(owner, rows)]
+        y[chunk, slot] = send(
             source,
             source,
             y_send_sem.at[chunk, slot],
@@ -516,23 +517,19 @@
             {"dp": device},
         )
 
-    d_values = mm(probs_low, d_att, ((0,), (0,)))
-    yv_all[mine] = (d_values * inverse).astype(jnp.bfloat16)
-    y = {}
-    for slot in (2, 0, 1, 3):
-        y[0, slot] = y_copy(yv_all, 0, me, slot, owners[slot])
+    def y_start(chunk, value):
+        y_all[chunk, mine] = (value * inverse).astype(jnp.bfloat16)
+        for slot in (2, 0, 1, 3):
+            y_copy(chunk, me, slot, owners[slot])
+
+    y_start(0, mm(probs_low, d_att, ((0,), (0,))))
     d_probs = mm(d_att, values, ((1,), (1,)))
     d_scores = (
         probs * (d_probs - jnp.sum(probs * d_probs, axis=1, keepdims=True))
     ).astype(jnp.bfloat16)
-    d_query = turn(mm(d_scores, key, ((1,), (0,))) * scale, -signed)
-    d_key = turn(mm(d_scores, query, ((0,), (0,))), -signed)
-    yqk_all[mine, :head] = (d_query * inverse).astype(jnp.bfloat16)
-    yqk_all[mine, head:] = (d_key * inverse).astype(jnp.bfloat16)
-    for slot in (2, 0, 1, 3):
-        y[1, slot] = y_copy(yqk_all, 1, me, slot, owners[slot])
-
-    out_total = out_part(me)
+    y_start(1, turn(mm(d_scores, key, ((1,), (0,))) * scale, -signed))
+    y_start(2, turn(mm(d_scores, query, ((0,), (0,))), -signed))
+
     x_turned[:, mine] = x_v[:, block(me, owned)].T
     for slot, source in enumerate((0, 1, 2, 3, 5, 4, 6)):
         columns[slot].wait_recv()
@@ -540,84 +537,91 @@
         x_turned[:, part] = x_all[part].T
 
     my_piece = pl.ds(pl.multiple_of(rep * piece, 16), piece)
-
-    def z_start(chunk, buf, received, total):
-        buf[...] = total.astype(jnp.bfloat16)
-        copies = []
+    r, g = {}, {}
+
+    def y_pass(chunk):
+        for slot, onward in ((2, 6), (0, 4), (1, 5)):
+            y[chunk, slot].wait_recv()
+            y_copy(chunk, owners[slot], onward, sibling)
+
+    def y_finish(chunk):
+        for slot in (3, 4, 5, 6):
+            y[chunk, slot].wait_recv()
+        total = mm(x_turned[...], y_all[chunk], ((1,), (0,)))
+        z_send[chunk] = total.astype(jnp.bfloat16)
         for off in range(1, replicas):
             peer = lax.rem(rep + off, replicas)
             part = pl.ds(pl.multiple_of(peer * piece, 16), piece)
-            copies.append(
-                send(
-                    buf.at[part],
-                    received.at[off - 1],
-                    r_send_sem.at[chunk, off],
-                    r_recv_sem.at[chunk, off],
-                    {"rep": peer},
-                )
+            r[chunk, off] = send(
+                z_send.at[chunk].at[part],
+                z_recv.at[chunk, off - 1],
+                r_send_sem.at[chunk, off],
+                r_recv_sem.at[chunk, off],
+                {"rep": peer},
             )
-        return copies
-
-    def z_middle(chunk, buf, received, gathered, copies):
-        whole = buf[my_piece].astype(jnp.float32)
+
+    def z_gather(chunk, whole):
+        z_all[chunk, my_piece] = (whole * (1.0 / replicas)).astype(jnp.bfloat16)
         for off in range(1, replicas):
-            copies[off - 1].wait_recv()
-            whole = whole + received[off - 1].astype(jnp.float32)
-        gathered[my_piece] = (whole * (1.0 / replicas)).astype(jnp.bfloat16)
-        last = []
+            g[chunk, off] = send(
+                z_all.at[chunk].at[my_piece],
+                z_all.at[chunk].at[my_piece],
+                g_send_sem.at[chunk, off],
+                g_recv_sem.at[chunk, off],
+                {"rep": lax.rem(rep + off, replicas)},
+            )
+
+    def z_sum(chunk):
+        whole = z_send[chunk, my_piece].astype(jnp.float32)
         for off in range(1, replicas):
-            peer = lax.rem(rep + off, replicas)
-            last.append(
-                send(
-                    gathered.at[my_piece],
-                    gathered.at[my_piece],
-                    g_send_sem.at[chunk, off],
-                    g_recv_sem.at[chunk, off],
-                    {"rep": peer},
-                )
+            r[chunk, off].wait_recv()
+            whole = whole + z_recv[chunk, off - 1].astype(jnp.float32)
+        z_gather(chunk, whole)
+
+    y_pass(0)
+    y_finish(0)
+    y_pass(1)
+    q_whole = p_send[:, rep].astype(jnp.float32)
+    for off in range(1, replicas):
+        p_copies[off - 1].wait_recv()
+        q_whole = q_whole + p_recv[off - 1].astype(jnp.float32)
+    q_send[...] = q_whole.astype(jnp.bfloat16)
+    q_copies = []
+    for slot in range(chips - 1):
+        q_copies.append(
+            send(
+                q_send.at[owners[slot] // CORES],
+                q_recv.at[slot],
+                q_send_sem.at[slot],
+                q_recv_sem.at[slot],
+                {"dp": owners[slot]},
             )
-        return last
-
-    def y_pass(buf, chunk):
-        for slot, onward in ((0, 4), (1, 5), (2, 6)):
-            y[chunk, slot].wait_recv()
-            y[chunk, onward] = y_copy(buf, chunk, owners[slot], onward, sibling)
-
-    y_pass(yv_all, 0)
-    for slot, copy in zip((2, 0, 1), p_copies):
-        copy.wait_recv()
-        out_total = out_total + p_recv[slot].astype(jnp.float32)
-    out_copies = z_start(0, zg_send, zg_recv, out_total)
-    for slot in (3, 4, 5, 6):
-        y[0, slot].wait_recv()
-    value_total = mm(x_turned[...], yv_all[...], ((1,), (0,)))
-    value_copies = z_start(1, zv_send, zv_recv, value_total)
-    y_pass(yqk_all, 1)
-    for slot in (3, 4, 5, 6):
-        y[1, slot].wait_recv()
-    both_total = mm(x_turned[...], yqk_all[...], ((1,), (0,)))
-    both_copies = z_start(2, zqk_send, zqk_recv, both_total)
-
-    out_last = z_middle(0, zg_send, zg_recv, zg_all, out_copies)
-    value_last = z_middle(1, zv_send, zv_recv, zv_all, value_copies)
-    both_last = z_middle(2, zqk_send, zqk_recv, zqk_all, both_copies)
-
+        )
+    y_finish(1)
+    y_pass(2)
+    y_finish(2)
+    whole = q_send[chip].astype(jnp.float32)
+    for slot in range(chips - 1):
+        q_copies[slot].wait_recv()
+        whole = whole + q_recv[slot].astype(jnp.float32)
+    z_gather(3, whole)
+    z_sum(0)
+    z_sum(1)
+    z_sum(2)
+
+    def gathered(chunk):
+        for off in range(1, replicas):
+            g[chunk, off].wait_recv()
+        return z_all[chunk].astype(jnp.float32)
+
+    go_ref[...] = gathered(3)
     wq_mine = wq_all.at[block(me, owned)]
-    for copy in out_last:
-        copy.wait_recv()
-    go_ref[...] = zg_all[...].astype(jnp.float32)
-    for copy in value_last:
-        copy.wait_recv()
-    value_sum = zv_all[...].astype(jnp.float32)
-    gq_ref[:, 2 * head :] = value_sum * gain_col
-    gain_sum = value_sum * wq_mine[:, 2 * head :].astype(jnp.float32)
-    for copy in both_last:
-        copy.wait_recv()
-    for place in range(2):
+    gain_sum = jnp.zeros((owned, head), jnp.float32)
+    for chunk, place in ((0, 2), (1, 0), (2, 1)):
         cols = pl.ds(place * head, head)
-        both_sum = zqk_all[:, cols].astype(jnp.float32)
-        gq_ref[:, cols] = both_sum * gain_col
-        gain_sum = gain_sum + both_sum * wq_mine[:, cols].astype(jnp.float32)
+        summed = gathered(chunk)
+        gq_ref[:, cols] = summed * gain_col
+        gain_sum = gain_sum + summed * wq_mine[:, cols].astype(jnp.float32)
     gg_ref[...] = to_row(jnp.sum(gain_sum, axis=1, keepdims=True))
     for copy in pending:
         copy.wait_send()
@@ -642,7 +646,7 @@
     chips = n // CORES
     piece = owned // replicas
     vmem = pl.BlockSpec(memory_space=pltpu.VMEM)
-    anywhere = pl.BlockSpec(memory_space=pl.ANY)
+    hbm = pl.BlockSpec(memory_space=pltpu.HBM)
     low = jnp.bfloat16
     sem = pltpu.SemaphoreType.DMA
     shapes = (
@@ -651,17 +655,10 @@
         jax.ShapeDtypeStruct((1, owned), jnp.float32),
     )
 
-    def z_buffers(cols):
-        return [
-            pltpu.VMEM((owned, cols), low),
-            pltpu.VMEM((replicas - 1, piece, cols), low),
-            pltpu.VMEM((owned, cols), low),
-        ]
-
     grads = pl.pallas_call(
         functools.partial(fused, n, replicas),
         out_shape=shapes,
-        in_specs=[anywhere] * 7,
+        in_specs=[hbm] * 7,
         out_specs=(vmem, vmem, vmem),
         scratch_shapes=[
             pltpu.VMEM((rows, width), low),
@@ -671,20 +668,21 @@
             pltpu.VMEM((owned,), low),
             pltpu.VMEM((width, wide), low),
             pltpu.VMEM((width, head), low),
-            pltpu.VMEM((n, 8, owned), jnp.float32),
+            pltpu.VMEM((n, 1, owned), jnp.float32),
             pltpu.VMEM((rows, width), low),
             pltpu.VMEM((chips, rows, owned), low),
             pltpu.VMEM((chips * owned, CORES * rows), low),
             pltpu.VMEM((CORES * rows, head), low),
             pltpu.VMEM((n * rows, owned), low),
             pltpu.VMEM((owned, n * rows), low),
-            pltpu.VMEM((n * rows, head), low),
-            pltpu.VMEM((n * rows, 2 * head), low),
-            pltpu.VMEM((chips - 1, owned, head), low),
-            pltpu.VMEM((chips - 1, owned, head), low),
-            *z_buffers(head),
-            *z_buffers(head),
-            *z_buffers(2 * head),
+            pltpu.VMEM((3, n * rows, head), low),
+            pltpu.VMEM((chips, replicas, piece, head), low),
+            pltpu.VMEM((replicas - 1, chips, piece, head), low),
+            pltpu.VMEM((chips, piece, head), low),
+            pltpu.VMEM((chips - 1, piece, head), low),
+            pltpu.VMEM((3, owned, head), low),
+            pltpu.VMEM((3, replicas - 1, piece, head), low),
+            pltpu.VMEM((4, owned, head), low),
             sem((7,)),
             sem((n - 1, 3)),
             sem((n - 1, 3)),
@@ -694,25 +692,33 @@
             sem((n - 1,)),
             sem((chips + 1,)),
             sem((chips + 1,)),
+            sem((replicas,)),
+            sem((replicas,)),
             sem((chips - 1,)),
             sem((chips - 1,)),
-            sem((2, n - 1)),
-            sem((2, n - 1)),
+            sem((3, n - 1)),
+            sem((3, n - 1)),
             sem((3, replicas)),
             sem((3, replicas)),
-            sem((3, replicas)),
-            sem((3, replicas)),
+            sem((4, replicas)),
+            sem((4, replicas)),
         ],
         compiler_params=pltpu.CompilerParams(
-            collective_id=0, has_side_effects=True, vmem_limit_bytes=60 * 1024 * 1024
+            collective_id=0, has_side_effects=True, vmem_limit_bytes=32 * 1024 * 1024
         ),
-    )(tokens, cotangent, doc_ids, valid_len, w_qkv, w_out, norm_gain)
+    )(
+        *(
+            pltpu.with_memory_space_constraint(array, pltpu.HBM)
+            for array in (tokens, cotangent, doc_ids, valid_len, w_qkv, w_out, norm_gain)
+        )
+    )
     grad_qkv, grad_out, grad_gain = pl.pallas_call(
         stored,
         out_shape=shapes,
         in_specs=[vmem] * 3,
-        out_specs=(anywhere,) * 3,
+        out_specs=(hbm,) * 3,
         scratch_shapes=[sem((3,))],
+        compiler_params=pltpu.CompilerParams(vmem_limit_bytes=4 * 1024 * 1024),
     )(*grads)
     return grad_qkv, grad_out, grad_gain.reshape(owned)
 

time: 50.4 us -> 45.5 us (0.903)
  Pallas kernels: 49.6 us -> 44.7 us
    pallas_call x1, Pallas kernels: 47.7 us -> 43.9 us  [one_kernel(): pl.pallas_call(functools.partial(fused, n, replicas), out_shape=shapes, i...]
    pallas_call x1, Pallas kernels: 1.88 us -> 0.82 us  [one_kernel(): pl.pallas_call(stored, out_shape=shapes, in_specs=[vmem] * 3, out_specs=(...]
where the time goes in v2:
time: 45.5 us; the launch traced here: 45.4 us
  Pallas kernels  44.7 us (98%)
  between operations  0.64 us (1%)
    pallas_call x1, Pallas kernels, one_kernel(): pl.pallas_call(functools.partial(fused, n, replicas), out_shape=shapes, i...  43.9 us

profile of v2, /device:TPU:0, one launch (start us, length us, event | category | flops | bytes accessed | tf_op | source)
XLA Modules:
  0.0 45.4 jit_solution(9369611674749874641)
XLA Ops:
  0.6 43.9 %shard_map.94 = (f32[256,384]{1,0:T(8,128)S(1)}, f32[256,128]{1,0:T(8,128)S(1)}, f32[1,256]{1,0:T(1,128)S(1)}) custom-call(bf16[128,2048]{1,0:T(8,128)(2,1)} %x_hbm.1, bf16[128,2048]{1,0:T(8,128)(2,1)} %dy_hbm.1, s32[2,64]{1,0:T(2,128)} %doc_hbm.1, s32[2]{0:T(128)} %valid_hbm.1, bf16[256,384]{1,0:T(8,128)(2,1)} %wq_hbm.1, bf16[256,128]{1,0:T(8,128)(2,1)} %wo_hbm.1, ...), custom_call_target="tpu_custom_call" | custom-call | tf_op jit(solution)/shard_map/pallas_call | solution.py:658
  44.5 0.8 %shard_map.95 = (f32[256,384]{1,0:T(8,128)}, f32[256,128]{1,0:T(8,128)}, f32[1,256]{1,0:T(1,128)}) custom-call(f32[256,384]{1,0:T(8,128)S(1)} %get-tuple-element.9.gq_ref, f32[256,128]{1,0:T(8,128)S(1)} %get-tuple-element.10.go_ref, f32[1,256]{1,0:T(1,128)S(1)} %get-tuple-element.11.gg_ref), custom_call_target="tpu_custom_call" | custom-call | tf_op jit(solution)/shard_map/pallas_call | solution.py:715

commit v3 on v2

--- a/solution.py
+++ b/solution.py
@@ -332,6 +332,17 @@
             {"dp": device},
         )
 
+    side = lax.rem(rep, 2)
+    partner = rep + 1 - 2 * side
+
+    def w_half(owner, part, which):
+        start = pl.multiple_of(owner * owned + which * half_owned, LANES)
+        return (wo_all if part == 2 else wq_all).at[pl.ds(start, half_owned)]
+
+    def half_copy(owner, part, which, slot, where):
+        source = w_half(owner, part, which)
+        return send(source, source, w_send_sem.at[slot, part], w_recv_sem.at[slot, part], where)
+
     loads[2].wait()
     gain_row = gain_v[...].reshape(1, owned).astype(jnp.float32)
     gain_all[me] = gain_row
@@ -339,11 +350,6 @@
     loads[1].wait()
     pl.semaphore_wait(barrier, n - 1 + replicas - 1)
 
-    w = {}
-    for part in range(2):
-        w[0, part] = w_copy(me, part, 0, owners[0])
-    for part in range(2):
-        w[3, part] = w_copy(me, part, 3, sibling)
     gains = {}
     for off in range(1, n):
         gains[off] = send(
@@ -353,6 +359,11 @@
             s_recv_sem.at[off],
             {"dp": lax.rem(me + off, n)},
         )
+    w = {}
+    for part in range(2):
+        w[0, part] = w_copy(me, part, 0, owners[0])
+    for part in range(2):
+        w[3, part] = w_copy(me, part, 3, sibling)
     w[3, 2] = w_copy(me, 2, 3, sibling)
 
     loads[4].wait()
@@ -397,9 +408,23 @@
     cosine = jnp.cos(angles)
     signed = jnp.sin(angles) * jnp.where(lane < head // 2, -1.0, 1.0)
 
-    for part in range(2):
-        w[1, part] = w_copy(me, part, 1, owners[1])
+    for part in (0, 2):
+        w[1, part] = half_copy(me, part, side, 1, {"dp": owners[1]})
     w[0, 2] = w_copy(me, 2, 0, owners[0])
+    mine = block(me, rows)
+    columns = {}
+
+    def x_copy(slot):
+        columns[slot] = send(
+            x_v.at[:, block(owners[slot], owned)],
+            x_all.at[mine],
+            a_send_sem.at[slot],
+            a_recv_sem.at[slot],
+            {"dp": owners[slot]},
+        )
+
+    for slot in (3,0,5,1):
+        x_copy(slot)
     for off in range(1, n):
         gains[off].wait_recv()
     for place in range(n):
@@ -420,10 +445,10 @@
         w[0, part].wait_recv()
         w[2, part] = w_copy(owners[0], part, 2, owners[1])
         w[4, part] = w_copy(owners[0], part, 4, sibling)
-    w[1, 2] = w_copy(me, 2, 1, owners[1])
-    for part in range(2):
+    for part in (0, 2):
         w[1, part].wait_recv()
-        w[5, part] = w_copy(owners[1], part, 5, sibling)
+        w[7, part] = half_copy(owners[1], part, side, 7, {"rep": partner})
+        w[5, part] = half_copy(owners[1], part, side, 5, {"dp": sibling})
 
     for place in range(chips):
         crossed[place].wait_recv()
@@ -432,35 +457,30 @@
         dy_turned[turned, rows:] = dy_sib[place].T
 
     total = times(owners[0], total)
-    total = times(owners[1], total)
 
     w[0, 2].wait_recv()
     w[2, 2] = w_copy(owners[0], 2, 2, owners[1])
     w[4, 2] = w_copy(owners[0], 2, 4, sibling)
-
-    mine = block(me, rows)
-    columns = {}
-    for slot in (2, 0, 1, 6, 5, 4, 3):
-        columns[slot] = send(
-            x_v.at[:, block(owners[slot], owned)],
-            x_all.at[mine],
-            a_send_sem.at[slot],
-            a_recv_sem.at[slot],
-            {"dp": owners[slot]},
-        )
-
-    for slot in (4, 5):
-        for part in range(2):
-            w[slot, part].wait_recv()
-        total = times(owners[slot], total)
+    for slot in (2,6,4):
+        x_copy(slot)
+
+    for part in range(2):
+        w[4, part].wait_recv()
+    total = times(owners[4], total)
     for part in range(2):
         w[2, part].wait_recv()
         w[6, part] = w_copy(owners[2], part, 6, sibling)
-    w[1, 2].wait_recv()
-    w[5, 2] = w_copy(owners[1], 2, 5, sibling)
+    for part in (0, 2):
+        w[7, part].wait_recv()
+        w[8, part] = half_copy(owners[1], part, 1 - side, 8, {"dp": sibling})
+
+    total = times(owners[1], total)
     total = times(owners[2], total)
     w[2, 2].wait_recv()
     w[6, 2] = w_copy(owners[2], 2, 6, sibling)
+    w[5, 0].wait_recv()
+    w[8, 0].wait_recv()
+    total = times(owners[5], total)
     for part in range(2):
         w[6, part].wait_recv()
     projected = times(owners[6], total)
@@ -485,7 +505,7 @@
         {"dp": sibling},
     )
 
-    for slot in (3, 4, 5, 6):
+    for slot in (3, 4, 5, 8, 6):
         w[slot, 2].wait_recv()
     d_att = (mm(dy_v[...], wo_all[...], ((1,), (0,))) * live_col).astype(jnp.bfloat16)
     att_copy.wait_recv()
@@ -579,8 +599,11 @@
         z_gather(chunk, whole)
 
     y_pass(0)
+    y_pass(1)
     y_finish(0)
-    y_pass(1)
+    y_pass(2)
+    y_finish(1)
+    y_finish(2)
     q_whole = p_send[:, rep].astype(jnp.float32)
     for off in range(1, replicas):
         p_copies[off - 1].wait_recv()
@@ -597,16 +620,13 @@
                 {"dp": owners[slot]},
             )
         )
-    y_finish(1)
-    y_pass(2)
-    y_finish(2)
+    z_sum(0)
+    z_sum(1)
     whole = q_send[chip].astype(jnp.float32)
     for slot in range(chips - 1):
         q_copies[slot].wait_recv()
         whole = whole + q_recv[slot].astype(jnp.float32)
     z_gather(3, whole)
-    z_sum(0)
-    z_sum(1)
     z_sum(2)
 
     def gathered(chunk):
@@ -614,7 +634,6 @@
             g[chunk, off].wait_recv()
         return z_all[chunk].astype(jnp.float32)
 
-    go_ref[...] = gathered(3)
     wq_mine = wq_all.at[block(me, owned)]
     gain_sum = jnp.zeros((owned, head), jnp.float32)
     for chunk, place in ((0, 2), (1, 0), (2, 1)):
@@ -622,6 +641,7 @@
         summed = gathered(chunk)
         gq_ref[:, cols] = summed * gain_col
         gain_sum = gain_sum + summed * wq_mine[:, cols].astype(jnp.float32)
+    go_ref[...] = gathered(3)
     gg_ref[...] = to_row(jnp.sum(gain_sum, axis=1, keepdims=True))
     for copy in pending:
         copy.wait_send()
@@ -684,8 +704,8 @@
             pltpu.VMEM((3, replicas - 1, piece, head), low),
             pltpu.VMEM((4, owned, head), low),
             sem((7,)),
-            sem((n - 1, 3)),
-            sem((n - 1, 3)),
+            sem((n + 1, 3)),
+            sem((n + 1, 3)),
             sem((n,)),
             sem((n,)),
             sem((n - 1,)),

time: 45.5 us -> 41.1 us (0.903)
  Pallas kernels: 44.7 us -> 40.3 us
    pallas_call x1, Pallas kernels: 43.9 us -> 39.5 us  [one_kernel(): pl.pallas_call(functools.partial(fused, n, replicas), out_shape=shapes, i...]
where the time goes in v3:
time: 41.1 us; the launch traced here: 40.9 us
  Pallas kernels  40.3 us (98%)
  between operations  0.64 us (2%)
    pallas_call x1, Pallas kernels, one_kernel(): pl.pallas_call(functools.partial(fused, n, replicas), out_shape=shapes, i...  39.5 us

profile of v3, /device:TPU:0, one launch (start us, length us, event | category | flops | bytes accessed | tf_op | source)
XLA Modules:
  0.0 40.9 jit_solution(12271473299204461000)
XLA Ops:
  0.6 39.5 %shard_map.94 = (f32[256,384]{1,0:T(8,128)S(1)}, f32[256,128]{1,0:T(8,128)S(1)}, f32[1,256]{1,0:T(1,128)S(1)}) custom-call(bf16[128,2048]{1,0:T(8,128)(2,1)} %x_hbm.1, bf16[128,2048]{1,0:T(8,128)(2,1)} %dy_hbm.1, s32[2,64]{1,0:T(2,128)} %doc_hbm.1, s32[2]{0:T(128)} %valid_hbm.1, bf16[256,384]{1,0:T(8,128)(2,1)} %wq_hbm.1, bf16[256,128]{1,0:T(8,128)(2,1)} %wo_hbm.1, ...), custom_call_target="tpu_custom_call" | custom-call | tf_op jit(solution)/shard_map/pallas_call | solution.py:678
  40.1 0.8 %shard_map.95 = (f32[256,384]{1,0:T(8,128)}, f32[256,128]{1,0:T(8,128)}, f32[1,256]{1,0:T(1,128)}) custom-call(f32[256,384]{1,0:T(8,128)S(1)} %get-tuple-element.9.gq_ref, f32[256,128]{1,0:T(8,128)S(1)} %get-tuple-element.10.go_ref, f32[1,256]{1,0:T(1,128)S(1)} %get-tuple-element.11.gg_ref), custom_call_target="tpu_custom_call" | custom-call | tf_op jit(solution)/shard_map/pallas_call | solution.py:735

commit v4 on v3

--- a/solution.py
+++ b/solution.py
@@ -220,25 +220,15 @@
     z_send,
     z_recv,
     z_all,
+    z_sums,
+    o_all,
     in_sem,
-    w_send_sem,
-    w_recv_sem,
-    s_send_sem,
-    s_recv_sem,
-    a_send_sem,
-    a_recv_sem,
-    d_send_sem,
-    d_recv_sem,
-    p_send_sem,
-    p_recv_sem,
-    q_send_sem,
-    q_recv_sem,
-    y_send_sem,
-    y_recv_sem,
-    r_send_sem,
-    r_recv_sem,
-    g_send_sem,
-    g_recv_sem,
+    sent_sem,
+    one_sem,
+    w_sem,
+    y_sem,
+    r_sem,
+    g_sem,
 ):
     me = lax.axis_index("dp")
     rep = lax.axis_index("rep")
@@ -285,20 +275,26 @@
             device_id_type=MESH,
         )
 
-    pending = []
-
-    def send(src, dst, send_sem, recv_sem, where):
-        copy = pltpu.make_async_remote_copy(
+    GAIN, X, DY, ATT, PARTS, PIECES, OUT, WQ, WO, Y, SUMS, DONE = range(12)
+
+    def remote(src, dst, group, recv_sem, where):
+        return pltpu.make_async_remote_copy(
             src_ref=src,
             dst_ref=dst,
-            send_sem=send_sem,
+            send_sem=sent_sem.at[group],
             recv_sem=recv_sem,
             device_id=where,
             device_id_type=MESH,
         )
-        copy.start()
-        pending.append(copy)
-        return copy
+
+    def send(src, dst, group, recv_sem, where):
+        remote(src, dst, group, recv_sem, where).start()
+
+    def landed(ref, recv_sem):
+        remote(ref, ref, 0, recv_sem, {"dp": sibling}).wait_recv()
+
+    def left(ref, group):
+        remote(ref, ref, group, one_sem.at[0], {"dp": sibling}).wait_send()
 
     along, across = lax.rem(chip, 2), chip // 2
     by_x = across * 2 + 1 - along
@@ -322,15 +318,41 @@
         start = pl.multiple_of(owner * owned + part * half_owned, LANES)
         return wq_all.at[pl.ds(start, half_owned)]
 
+    arrivals = {
+        (0, 0): 0,
+        (0, 1): 1,
+        (0, 2): 2,
+        (1, 0): 3,
+        (1, 2): 4,
+        (2, 0): 5,
+        (2, 1): 6,
+        (2, 2): 7,
+        (3, 0): 8,
+        (3, 1): 8,
+        (4, 0): 9,
+        (4, 1): 9,
+        (5, 0): 10,
+        (8, 0): 10,
+        (6, 0): 11,
+        (6, 1): 11,
+        (7, 0): 12,
+        (7, 2): 13,
+        (3, 2): 14,
+        (4, 2): 14,
+        (5, 2): 14,
+        (8, 2): 14,
+        (6, 2): 14,
+    }
+
+    def w_send(source, slot, part, where):
+        group = WO if part == 2 else WQ
+        send(source, source, group, w_sem.at[arrivals[slot, part]], where)
+
     def w_copy(owner, part, slot, device):
-        source = w_part(owner, part)
-        return send(
-            source,
-            source,
-            w_send_sem.at[slot, part],
-            w_recv_sem.at[slot, part],
-            {"dp": device},
-        )
+        w_send(w_part(owner, part), slot, part, {"dp": device})
+
+    def w_landed(slot, part, size):
+        landed((wo_all if part == 2 else wq_all).at[:size], w_sem.at[arrivals[slot, part]])
 
     side = lax.rem(rep, 2)
     partner = rep + 1 - 2 * side
@@ -340,8 +362,7 @@
         return (wo_all if part == 2 else wq_all).at[pl.ds(start, half_owned)]
 
     def half_copy(owner, part, which, slot, where):
-        source = w_half(owner, part, which)
-        return send(source, source, w_send_sem.at[slot, part], w_recv_sem.at[slot, part], where)
+        w_send(w_half(owner, part, which), slot, part, where)
 
     loads[2].wait()
     gain_row = gain_v[...].reshape(1, owned).astype(jnp.float32)
@@ -350,33 +371,28 @@
     loads[1].wait()
     pl.semaphore_wait(barrier, n - 1 + replicas - 1)
 
-    gains = {}
     for off in range(1, n):
-        gains[off] = send(
+        send(
             gain_all.at[me],
             gain_all.at[me],
-            s_send_sem.at[off],
-            s_recv_sem.at[off],
+            GAIN,
+            one_sem.at[GAIN],
             {"dp": lax.rem(me + off, n)},
         )
-    w = {}
     for part in range(2):
-        w[0, part] = w_copy(me, part, 0, owners[0])
+        w_copy(me, part, 0, owners[0])
     for part in range(2):
-        w[3, part] = w_copy(me, part, 3, sibling)
-    w[3, 2] = w_copy(me, 2, 3, sibling)
+        w_copy(me, part, 3, sibling)
+    w_copy(me, 2, 3, sibling)
 
     loads[4].wait()
-    crossed = []
     for place in range(chips):
-        crossed.append(
-            send(
-                dy_v.at[:, block(place * CORES + 1 - core, owned)],
-                dy_sib.at[place],
-                d_send_sem.at[place],
-                d_recv_sem.at[place],
-                {"dp": sibling},
-            )
+        send(
+            dy_v.at[:, block(place * CORES + 1 - core, owned)],
+            dy_sib.at[place],
+            DY,
+            one_sem.at[DY],
+            {"dp": sibling},
         )
 
     loads[3].wait()
@@ -409,24 +425,22 @@
     signed = jnp.sin(angles) * jnp.where(lane < head // 2, -1.0, 1.0)
 
     for part in (0, 2):
-        w[1, part] = half_copy(me, part, side, 1, {"dp": owners[1]})
-    w[0, 2] = w_copy(me, 2, 0, owners[0])
+        half_copy(me, part, side, 1, {"dp": owners[1]})
+    w_copy(me, 2, 0, owners[0])
     mine = block(me, rows)
-    columns = {}
 
     def x_copy(slot):
-        columns[slot] = send(
+        send(
             x_v.at[:, block(owners[slot], owned)],
             x_all.at[mine],
-            a_send_sem.at[slot],
-            a_recv_sem.at[slot],
+            X,
+            one_sem.at[X],
             {"dp": owners[slot]},
         )
 
-    for slot in (3,0,5,1):
+    for slot in (3, 0, 5, 1):
         x_copy(slot)
-    for off in range(1, n):
-        gains[off].wait_recv()
+    landed(gain_all.at[: n - 1], one_sem.at[GAIN])
     for place in range(n):
         cols = pl.ds(place * owned, owned)
         scaled = x_v[:, cols].astype(jnp.float32) * inverse
@@ -437,52 +451,48 @@
         return product if total is None else total + product
 
     total = times(me, None)
-    w[3, 0].wait_recv()
-    w[3, 1].wait_recv()
+    w_landed(3, 0, owned)
     total = times(sibling, total)
 
     for part in range(2):
-        w[0, part].wait_recv()
-        w[2, part] = w_copy(owners[0], part, 2, owners[1])
-        w[4, part] = w_copy(owners[0], part, 4, sibling)
+        w_landed(0, part, half_owned)
+        w_copy(owners[0], part, 2, owners[1])
+        w_copy(owners[0], part, 4, sibling)
     for part in (0, 2):
-        w[1, part].wait_recv()
-        w[7, part] = half_copy(owners[1], part, side, 7, {"rep": partner})
-        w[5, part] = half_copy(owners[1], part, side, 5, {"dp": sibling})
-
+        w_landed(1, part, half_owned)
+        half_copy(owners[1], part, side, 7, {"rep": partner})
+        half_copy(owners[1], part, side, 5, {"dp": sibling})
+
+    landed(dy_sib, one_sem.at[DY])
     for place in range(chips):
-        crossed[place].wait_recv()
         turned = pl.ds(place * owned, owned)
         dy_turned[turned, :rows] = dy_v[:, block(place * CORES + core, owned)].T
         dy_turned[turned, rows:] = dy_sib[place].T
 
     total = times(owners[0], total)
 
-    w[0, 2].wait_recv()
-    w[2, 2] = w_copy(owners[0], 2, 2, owners[1])
-    w[4, 2] = w_copy(owners[0], 2, 4, sibling)
-    for slot in (2,6,4):
+    w_landed(0, 2, owned)
+    w_copy(owners[0], 2, 2, owners[1])
+    w_copy(owners[0], 2, 4, sibling)
+    for slot in (2, 6, 4):
         x_copy(slot)
 
-    for part in range(2):
-        w[4, part].wait_recv()
+    w_landed(4, 0, owned)
     total = times(owners[4], total)
     for part in range(2):
-        w[2, part].wait_recv()
-        w[6, part] = w_copy(owners[2], part, 6, sibling)
+        w_landed(2, part, half_owned)
+        w_copy(owners[2], part, 6, sibling)
     for part in (0, 2):
-        w[7, part].wait_recv()
-        w[8, part] = half_copy(owners[1], part, 1 - side, 8, {"dp": sibling})
+        w_landed(7, part, half_owned)
+        half_copy(owners[1], part, 1 - side, 8, {"dp": sibling})
 
     total = times(owners[1], total)
     total = times(owners[2], total)
-    w[2, 2].wait_recv()
-    w[6, 2] = w_copy(owners[2], 2, 6, sibling)
-    w[5, 0].wait_recv()
-    w[8, 0].wait_recv()
+    w_landed(2, 2, owned)
+    w_copy(owners[2], 2, 6, sibling)
+    w_landed(5, 0, owned)
     total = times(owners[5], total)
-    for part in range(2):
-        w[6, part].wait_recv()
+    w_landed(6, 0, owned)
     projected = times(owners[6], total)
 
     def turn(vector, sine_part):
@@ -497,45 +507,20 @@
     probs_low = probs.astype(jnp.bfloat16)
     attended = mm(probs_low, values, ((1,), (0,)))
     att[:rows] = (attended * live_col).astype(jnp.bfloat16)
-    att_copy = send(
-        att.at[:rows],
-        att.at[rows:],
-        d_send_sem.at[chips],
-        d_recv_sem.at[chips],
-        {"dp": sibling},
-    )
-
-    for slot in (3, 4, 5, 8, 6):
-        w[slot, 2].wait_recv()
+    send(att.at[:rows], att.at[rows:], ATT, one_sem.at[ATT], {"dp": sibling})
+    w_landed(3, 2, chips * owned)
     d_att = (mm(dy_v[...], wo_all[...], ((1,), (0,))) * live_col).astype(jnp.bfloat16)
-    att_copy.wait_recv()
+    landed(att.at[rows:], one_sem.at[ATT])
 
     by_chip = mm(dy_turned[...], att[...], ((1,), (0,)))
     p_send[...] = by_chip.reshape(chips, replicas, piece, head).astype(jnp.bfloat16)
-    p_copies = []
     for off in range(1, replicas):
         peer = lax.rem(rep + off, replicas)
-        p_copies.append(
-            send(
-                p_send.at[:, peer],
-                p_recv.at[off - 1],
-                p_send_sem.at[off],
-                p_recv_sem.at[off],
-                {"rep": peer},
-            )
-        )
-
-    y = {}
+        send(p_send.at[:, peer], p_recv.at[off - 1], PARTS, one_sem.at[PARTS], {"rep": peer})
 
     def y_copy(chunk, owner, slot, device):
         source = y_all.at[chunk].at[block(owner, rows)]
-        y[chunk, slot] = send(
-            source,
-            source,
-            y_send_sem.at[chunk, slot],
-            y_recv_sem.at[chunk, slot],
-            {"dp": device},
-        )
+        send(source, source, Y, y_sem.at[chunk, min(slot, 3)], {"dp": device})
 
     def y_start(chunk, value):
         y_all[chunk, mine] = (value * inverse).astype(jnp.bfloat16)
@@ -551,52 +536,98 @@
     y_start(2, turn(mm(d_scores, query, ((0,), (0,))), -signed))
 
     x_turned[:, mine] = x_v[:, block(me, owned)].T
-    for slot, source in enumerate((0, 1, 2, 3, 5, 4, 6)):
-        columns[slot].wait_recv()
-        part = block(owners[source], rows)
+    landed(x_all.at[: (n - 1) * rows], one_sem.at[X])
+    for owner in owners:
+        part = block(owner, rows)
         x_turned[:, part] = x_all[part].T
 
     my_piece = pl.ds(pl.multiple_of(rep * piece, 16), piece)
-    r, g = {}, {}
 
     def y_pass(chunk):
         for slot, onward in ((2, 6), (0, 4), (1, 5)):
-            y[chunk, slot].wait_recv()
+            landed(y_all.at[chunk].at[:rows], y_sem.at[chunk, slot])
             y_copy(chunk, owners[slot], onward, sibling)
 
+    lead = replicas // 2 - 1
+    near = rep // (replicas // 2)
+    central = (rep == lead) | (rep == lead + 1)
+    summing = central & (core == 1)
+    head_core = chip * CORES + 1
+
+    def half_rows(which):
+        return pl.ds(pl.multiple_of(which * half_owned, LANES), half_owned)
+
+    def to_center(chunk, which):
+        send(
+            z_send.at[chunk].at[half_rows(which)],
+            z_recv.at[chunk, core, rep],
+            SUMS,
+            r_sem.at[chunk, core],
+            {"dp": head_core, "rep": lead + which},
+        )
+
     def y_finish(chunk):
-        for slot in (3, 4, 5, 6):
-            y[chunk, slot].wait_recv()
+        landed(y_all.at[chunk].at[: chips * rows], y_sem.at[chunk, 3])
         total = mm(x_turned[...], y_all[chunk], ((1,), (0,)))
         z_send[chunk] = total.astype(jnp.bfloat16)
+        to_center(chunk, 1 - near)
+
+        @pl.when(jnp.logical_not(summing))
+        def _():
+            to_center(chunk, near)
+
+    def z_gather(whole):
+        o_all[my_piece] = (whole * (1.0 / replicas)).astype(jnp.bfloat16)
         for off in range(1, replicas):
-            peer = lax.rem(rep + off, replicas)
-            part = pl.ds(pl.multiple_of(peer * piece, 16), piece)
-            r[chunk, off] = send(
-                z_send.at[chunk].at[part],
-                z_recv.at[chunk, off - 1],
-                r_send_sem.at[chunk, off],
-                r_recv_sem.at[chunk, off],
-                {"rep": peer},
-            )
-
-    def z_gather(chunk, whole):
-        z_all[chunk, my_piece] = (whole * (1.0 / replicas)).astype(jnp.bfloat16)
-        for off in range(1, replicas):
-            g[chunk, off] = send(
-                z_all.at[chunk].at[my_piece],
-                z_all.at[chunk].at[my_piece],
-                g_send_sem.at[chunk, off],
-                g_recv_sem.at[chunk, off],
+            send(
+                o_all.at[my_piece],
+                o_all.at[my_piece],
+                OUT,
+                one_sem.at[OUT],
                 {"rep": lax.rem(rep + off, replicas)},
             )
 
+    def from_center(chunk, place, off):
+        rows_here = z_all.at[chunk].at[half_rows(near)]
+        send(
+            rows_here if place == 1 else z_sums.at[chunk],
+            rows_here,
+            DONE,
+            g_sem.at[chunk, near],
+            {"dp": chip * CORES + place, "rep": lax.rem(rep + off, replicas)},
+        )
+
     def z_sum(chunk):
-        whole = z_send[chunk, my_piece].astype(jnp.float32)
-        for off in range(1, replicas):
-            r[chunk, off].wait_recv()
-            whole = whole + z_recv[chunk, off - 1].astype(jnp.float32)
-        z_gather(chunk, whole)
+        @pl.when(summing)
+        def _():
+            for place in range(CORES):
+                if place == 1:
+                    landed(z_recv.at[chunk, 1].at[: replicas - 1], r_sem.at[chunk, 1])
+                    whole = z_send[chunk, half_rows(near)].astype(jnp.float32)
+                else:
+                    landed(z_recv.at[chunk, 0], r_sem.at[chunk, 0])
+                    whole = z_recv[chunk, 0, rep].astype(jnp.float32)
+                for off in range(1, replicas):
+                    source = lax.rem(rep + off, replicas)
+                    whole = whole + z_recv[chunk, place, source].astype(jnp.float32)
+                low = (whole * (1.0 / replicas)).astype(jnp.bfloat16)
+                if place == 1:
+                    z_all[chunk, half_rows(near)] = low
+                else:
+                    z_sums[chunk] = low
+                for off in (2, 3, 1) if place == 1 else (2, 3, 1, 0):
+                    from_center(chunk, place, off)
+
+    def z_arrived(chunk, which):
+        landed(z_all.at[chunk].at[:half_owned], g_sem.at[chunk, which])
+
+    def z_done(chunk):
+        @pl.when(jnp.logical_not(summing))
+        def _():
+            z_arrived(chunk, near)
+
+        z_arrived(chunk, 1 - near)
+        return z_all[chunk].astype(jnp.float32)
 
     y_pass(0)
     y_pass(1)
@@ -605,46 +636,59 @@
     y_finish(1)
     y_finish(2)
     q_whole = p_send[:, rep].astype(jnp.float32)
+    landed(p_recv, one_sem.at[PARTS])
     for off in range(1, replicas):
-        p_copies[off - 1].wait_recv()
         q_whole = q_whole + p_recv[off - 1].astype(jnp.float32)
     q_send[...] = q_whole.astype(jnp.bfloat16)
-    q_copies = []
     for slot in range(chips - 1):
-        q_copies.append(
-            send(
-                q_send.at[owners[slot] // CORES],
-                q_recv.at[slot],
-                q_send_sem.at[slot],
-                q_recv_sem.at[slot],
-                {"dp": owners[slot]},
-            )
+        send(
+            q_send.at[owners[slot] // CORES],
+            q_recv.at[slot],
+            PIECES,
+            one_sem.at[PIECES],
+            {"dp": owners[slot]},
         )
     z_sum(0)
     z_sum(1)
     whole = q_send[chip].astype(jnp.float32)
+    landed(q_recv, one_sem.at[PIECES])
     for slot in range(chips - 1):
-        q_copies[slot].wait_recv()
         whole = whole + q_recv[slot].astype(jnp.float32)
-    z_gather(3, whole)
+    z_gather(whole)
     z_sum(2)
-
-    def gathered(chunk):
-        for off in range(1, replicas):
-            g[chunk, off].wait_recv()
-        return z_all[chunk].astype(jnp.float32)
+    others = (n - 1) * owned
+    left(gain_all.at[: n - 1], GAIN)
+    left(x_all.at[: (n - 1) * rows], X)
+    left(dy_sib, DY)
+    left(att.at[rows:], ATT)
+    left(p_recv, PARTS)
+    left(q_recv, PIECES)
+    left(wq_all.at[:others], WQ)
+    left(wo_all.at[:others], WO)
+    left(y_all.at[:, : (n - 1) * rows], Y)
 
     wq_mine = wq_all.at[block(me, owned)]
-    gain_sum = jnp.zeros((owned, head), jnp.float32)
+    gain_sum = None
     for chunk, place in ((0, 2), (1, 0), (2, 1)):
+        if chunk == 2:
+            landed(o_all.at[: (replicas - 1) * piece], one_sem.at[OUT])
+            go_ref[...] = o_all[...].astype(jnp.float32)
         cols = pl.ds(place * head, head)
-        summed = gathered(chunk)
+        summed = z_done(chunk)
         gq_ref[:, cols] = summed * gain_col
-        gain_sum = gain_sum + summed * wq_mine[:, cols].astype(jnp.float32)
-    go_ref[...] = gathered(3)
+        term = summed * wq_mine[:, cols].astype(jnp.float32)
+        gain_sum = term if gain_sum is None else gain_sum + term
     gg_ref[...] = to_row(jnp.sum(gain_sum, axis=1, keepdims=True))
-    for copy in pending:
-        copy.wait_send()
+    left(o_all.at[: (replicas - 1) * piece], OUT)
+
+    @pl.when(jnp.logical_not(summing))
+    def _():
+        left(z_send, SUMS)
+
+    @pl.when(summing)
+    def _():
+        left(z_send.at[:, :half_owned], SUMS)
+        left(y_all.at[:, : (2 * replicas - 1) * half_owned], DONE)
 
 
 def stored(gq_ref, go_ref, gg_ref, gq_out, go_out, gg_out, sem):
@@ -701,27 +745,17 @@
             pltpu.VMEM((chips, piece, head), low),
             pltpu.VMEM((chips - 1, piece, head), low),
             pltpu.VMEM((3, owned, head), low),
-            pltpu.VMEM((3, replicas - 1, piece, head), low),
-            pltpu.VMEM((4, owned, head), low),
+            pltpu.VMEM((3, CORES, replicas, owned // 2, head), low),
+            pltpu.VMEM((3, owned, head), low),
+            pltpu.VMEM((3, owned // 2, head), low),
+            pltpu.VMEM((owned, head), low),
             sem((7,)),
-            sem((n + 1, 3)),
-            sem((n + 1, 3)),
-            sem((n,)),
-            sem((n,)),
-            sem((n - 1,)),
-            sem((n - 1,)),
-            sem((chips + 1,)),
-            sem((chips + 1,)),
-            sem((replicas,)),
-            sem((replicas,)),
-            sem((chips - 1,)),
-            sem((chips - 1,)),
-            sem((3, n - 1)),
-            sem((3, n - 1)),
-            sem((3, replicas)),
-            sem((3, replicas)),
-            sem((4, replicas)),
-            sem((4, replicas)),
+            sem((12,)),
+            sem((7,)),
+            sem((15,)),
+            sem((3, 4)),
+            sem((3, CORES)),
+            sem((3, 2)),
         ],
         compiler_params=pltpu.CompilerParams(
             collective_id=0, has_side_effects=True, vmem_limit_bytes=32 * 1024 * 1024
@@ -749,9 +783,9 @@
     rows, owned, head = tokens.shape[0], w_qkv.shape[0], w_out.shape[1]
     fits = (
         n == 4 * CORES
-        and replicas > 1
+        and replicas == 4
         and owned % LANES == 0
-        and owned % (16 * replicas) == 0
+        and owned % (2 * LANES) == 0
         and rows % LANES == 0
         and rows * n <= 2048
         and head == LANES

time: 41.1 us -> 38.8 us (0.944)
  Pallas kernels: 40.3 us -> 38 us
    pallas_call x1, Pallas kernels: 39.5 us -> 37.2 us  [one_kernel(): pl.pallas_call(functools.partial(fused, n, replicas), out_shape=shapes, i...]
where the time goes in v4:
time: 38.8 us; the launch traced here: 38.6 us
  Pallas kernels  38 us (98%)
  between operations  0.64 us (2%)
    pallas_call x1, Pallas kernels, one_kernel(): pl.pallas_call(functools.partial(fused, n, replicas), out_shape=shapes, i...  37.2 us
    pallas_call x1, Pallas kernels, one_kernel(): pl.pallas_call(stored, out_shape=shapes, in_specs=[vmem] * 3, out_specs=(...  0.82 us

profile of v4, /device:TPU:0, one launch (start us, length us, event | category | flops | bytes accessed | tf_op | source)
XLA Modules:
  0.0 38.6 jit_solution(5714874679325537235)
XLA Ops:
  0.6 37.2 %shard_map.94 = (f32[256,384]{1,0:T(8,128)S(1)}, f32[256,128]{1,0:T(8,128)S(1)}, f32[1,256]{1,0:T(1,128)S(1)}) custom-call(bf16[128,2048]{1,0:T(8,128)(2,1)} %x_hbm.1, bf16[128,2048]{1,0:T(8,128)(2,1)} %dy_hbm.1, s32[2,64]{1,0:T(2,128)} %doc_hbm.1, s32[2]{0:T(128)} %valid_hbm.1, bf16[256,384]{1,0:T(8,128)(2,1)} %wq_hbm.1, bf16[256,128]{1,0:T(8,128)(2,1)} %wo_hbm.1, ...), custom_call_target="tpu_custom_call" | custom-call | tf_op jit(solution)/shard_map/pallas_call | solution.py:722
  37.8 0.8 %shard_map.95 = (f32[256,384]{1,0:T(8,128)}, f32[256,128]{1,0:T(8,128)}, f32[1,256]{1,0:T(1,128)}) custom-call(f32[256,384]{1,0:T(8,128)S(1)} %get-tuple-element.9.gq_ref, f32[256,128]{1,0:T(8,128)S(1)} %get-tuple-element.10.go_ref, f32[1,256]{1,0:T(1,128)S(1)} %get-tuple-element.11.gg_ref), custom_call_target="tpu_custom_call" | custom-call | tf_op jit(solution)/shard_map/pallas_call | solution.py:769
